TPU v7x, 32 devices: a 4x4x1 block of a 4x4x8 slice. The times are simulated.
32 devices in a mesh: dp: 1 (over z), cp: 4 (over y), tp: 8 (over x, core).
Axes of the slice: x: 4, y: 4, z: 1, core: 2. Of those that a mesh axis runs over, the one named last changes fastest.
The devices are a block of a 4x4x8 slice.
Arguments:
- x: bfloat16 [8192, 2048], P(('dp', 'cp', 'tp'))
- idx: int32 [8192, 2], P(('dp', 'cp', 'tp'))
- gates: float32 [8192, 2], P(('dp', 'cp', 'tp'))
- wq: bfloat16 [2048, 2048], P(None, 'tp')
- wk: bfloat16 [2048, 2048], P(None, 'tp')
- wv: bfloat16 [2048, 2048], P(None, 'tp')
- wo: bfloat16 [2048, 2048], P('tp')
- w1g: bfloat16 [32, 2048, 1024], P(('cp', 'tp'))
- w1u: bfloat16 [32, 2048, 1024], P(('cp', 'tp'))
- w2: bfloat16 [32, 1024, 2048], P(('cp', 'tp'))
Outputs:
- output: bfloat16 [8192, 2048], P(('dp', 'cp', 'tp'))
All inputs are finite; a program needn't handle non-finite values.
Results may differ from a plain program's by a relative error of at most 0.010004.
Values are sent between devices in bfloat16 or wider.
A program may use at most 768 MiB of HBM per device.

v0:
```python
import jax
import jax.numpy as jnp
from jax import lax
from jax.sharding import PartitionSpec as P

HEAD_DIM = 128
NEG = -1e30


def expert_ffn(rows, wg, wu, wd):
    gg = jnp.dot(rows, wg, preferred_element_type=jnp.float32)
    uu = jnp.dot(rows, wu, preferred_element_type=jnp.float32)
    act = (jax.nn.silu(gg) * uu).astype(jnp.bfloat16)
    return jnp.dot(act, wd, preferred_element_type=jnp.float32).astype(jnp.bfloat16)


def attention_residual(x, wq, wk, wv, wo, cp):
    rank = lax.axis_index('cp')
    xs = lax.all_gather(x, 'tp', axis=0, tiled=True)
    n = xs.shape[0]
    seg = n // 2
    q = jnp.dot(xs, wq, preferred_element_type=jnp.float32).astype(jnp.bfloat16)
    k = jnp.dot(xs, wk, preferred_element_type=jnp.float32).astype(jnp.bfloat16)
    v = jnp.dot(xs, wv, preferred_element_type=jnp.float32).astype(jnp.bfloat16)
    hq = q.shape[1] // HEAD_DIM
    hkvv = k.shape[1] // HEAD_DIM
    g = hq // hkvv
    kvs = lax.all_gather(jnp.concatenate([k, v], axis=1), 'cp', axis=0)
    rows = jnp.arange(n)

    def positions(src):
        s_id = jnp.where(rows < seg, src, 2 * cp - 1 - src)
        return s_id * seg + rows % seg

    qpos = positions(rank)
    q4 = q.reshape(n, hkvv, g, HEAD_DIM)
    scale = HEAD_DIM ** -0.5
    m = jnp.full((hkvv, g, n), NEG, jnp.float32)
    l = jnp.zeros((hkvv, g, n), jnp.float32)
    acc = jnp.zeros((hkvv, g, n, HEAD_DIM), jnp.float32)
    for j in range(cp):
        kj = kvs[j, :, :hkvv * HEAD_DIM].reshape(n, hkvv, HEAD_DIM)
        vj = kvs[j, :, hkvv * HEAD_DIM:].reshape(n, hkvv, HEAD_DIM)
        mask = positions(j)[None, :] <= qpos[:, None]
        s = jnp.einsum('nkgd,mkd->kgnm', q4, kj, preferred_element_type=jnp.float32) * scale
        s = jnp.where(mask, s, NEG)
        mn = jnp.maximum(m, jnp.max(s, axis=-1))
        w = jnp.where(mask, jnp.exp(s - mn[:, :, :, None]), 0.0)
        c = jnp.exp(m - mn)
        l = l * c + jnp.sum(w, axis=-1)
        acc = acc * c[:, :, :, None] + jnp.einsum('kgnm,mkd->kgnd', w.astype(jnp.bfloat16), vj, preferred_element_type=jnp.float32)
        m = mn
    o = (acc / l[:, :, :, None]).transpose(2, 0, 1, 3).reshape(n, hq * HEAD_DIM).astype(jnp.bfloat16)
    part = jnp.dot(o, wo, preferred_element_type=jnp.float32)
    att = lax.psum_scatter(part, 'tp', scatter_dimension=0, tiled=True)
    return (x.astype(jnp.float32) + att).astype(jnp.bfloat16)


def solution(mesh):
    cp = mesh.shape['cp']
    tp = mesh.shape['tp']
    ne = cp * tp
    rows_spec = P(('dp', 'cp', 'tp'), None)
    exp_spec = P(('cp', 'tp'), None, None)

    def local(x, idx, gates, wq, wk, wv, wo, w1g, w1u, w2):
        h = attention_residual(x, wq, wk, wv, wo, cp)
        t, hd = h.shape
        kk = idx.shape[1]
        cap = 4 * t // ne
        ea = idx.reshape(-1)
        tok = jnp.arange(t * kk) // kk
        onehot = (ea[:, None] == jnp.arange(ne)[None, :]).astype(jnp.int32)
        slot = jnp.take_along_axis(jnp.cumsum(onehot, axis=0), ea[:, None], axis=1)[:, 0] - 1
        send = jnp.zeros((ne, cap, hd), jnp.bfloat16).at[ea, slot].set(h[tok])
        recv = lax.all_to_all(send, ('cp', 'tp'), 0, 0, tiled=True)
        z = expert_ffn(recv.reshape(ne * cap, hd), w1g[0], w1u[0], w2[0])
        back = lax.all_to_all(z.reshape(ne, cap, hd), ('cp', 'tp'), 0, 0, tiled=True)
        zt = back[ea, slot].astype(jnp.float32).reshape(t, kk, hd)
        y = h.astype(jnp.float32) + jnp.sum(gates[:, :, None] * zt, axis=1)
        return y.astype(jnp.bfloat16)

    return jax.shard_map(local, mesh=mesh, in_specs=(rows_spec, rows_spec, rows_spec, P(None, 'tp'), P(None, 'tp'), P(None, 'tp'), P('tp', None), exp_spec, exp_spec, exp_spec), out_specs=rows_spec, check_vma=False)
```

profile of v0, /device:TPU:111, one launch (start us, length us, event | category | flops | bytes accessed | tf_op | source)
XLA Modules:
  0.0 756.3 jit_solution(6691895866911306301)
XLA Ops:
  6.6 0.7 all-gather.4.cloned.1.call-update
  7.3 0.1 all-gather.6.cloned.1.call-start
  7.4 49.3 %all-gather.4.cloned.1.call-done = bf16[2048,2048]{1,0:T(8,128)(2,1)} async-done(((bf16[256,2048]{1,0:T(8,128)(2,1)}), bf16[2048,2048]{1,0:T(8,128)(2,1)}) %all-gather.4.cloned.1.call-update) | async-done | bytes 8388624 | tf_op jit(solution)/shard_map/all_gather | solution.py:19
  56.7 6.1 convolution_convert_fusion.1
  62.9 2.4 convolution_convert_fusion.2
  65.3 1.5 pad_maximum_fusion
  66.7 0.1 all-gather.6.cloned.1.call-update
  66.8 0.4 reduce-scatter.2.cloned.1.call-start
  67.2 0.0 copy-start.13
  67.3 10.5 %broadcast_compare_fusion.3 = (pred[2048,2048]{0,1:T(8,128)(4,1)}, pred[2048,2048]{0,1:T(8,128)(4,1)}, pred[2048,2048]{0,1:T(8,128)(4,1)}, pred[2048,2048]{0,1:T(8,128)(4,1)}) fusion(s32[2048]{0:T(1024)S(1)} %fusion.73, s32[2048]{0:T(1024)S(1)} %fusion.74, s32[2048]{0:T(1024)S(1)} %fusion.72, s32[2048]{0:T(1024)S(1)} %fusion.71, s32[2048]{0:T(1024)S(1)} %fusion.70), kind=kLoop, calls=%fused_computation.39 | loop fusion | flops 16777216 | bytes 16818176 | tf_op jit(solution)/shard_map/le | solution.py:44
  77.7 6.7 convolution_convert_fusion
  84.5 64.5 %all-gather.6.cloned.1.call-done = bf16[8192,512]{0,1:T(8,128)(2,1)} async-done(((bf16[2048,512]{0,1:T(8,128)(2,1)}), bf16[8192,512]{0,1:T(8,128)(2,1)}) %all-gather.6.cloned.1.call-update) | async-done | bytes 8388624 | tf_op jit(solution)/shard_map/all_gather | solution.py:28
  149.0 14.6 %reshape.517 = bf16[4,2048,512]{1,0,2:T(4,128)(2,1)} reshape(bf16[8192,512]{0,1:T(8,128)(2,1)} %all-gather.6.cloned.1.call-done) | data formatting | bytes 16777216 | tf_op jit(solution)/shard_map/all_gather | solution.py:28
  163.5 24.3 %fusion.101 = (bf16[1,2048,256]{1,0,2:T(2,128)(2,1)S(1)}, bf16[1,2048,256]{1,0,2:T(2,128)(2,1)S(1)}, bf16[1,2048,256]{1,0,2:T(2,128)(2,1)S(1)}, bf16[1,2048,256]...) fusion(bf16[4,2048,512]{1,0,2:T(4,128)(2,1)} %reshape.517), kind=kLoop, calls=%fused_computation.129 | loop fusion | bytes 16777216 | tf_op jit(solution)/shard_map/slice | solution.py:43
  187.9 1.6 copy.57
  189.5 1.6 copy.63
  191.0 1.6 copy.61
  192.6 1.6 copy.59
  194.3 1.6 copy.58
  195.8 1.6 copy.60
  197.4 0.6 copy.62
  198.0 1.6 copy.64
  199.6 16.6 %fusion = (f32[2,2048]{1,0:T(2,128)S(1)}, f32[2,2048,2048]{2,1,0:T(8,128)}) fusion(pred[2048,2048]{0,1:T(8,128)(4,1)} %get-tuple-element.24, bf16[2048,2,128]{0,2,1:T(8,128)(2,1)} %bitcast.185, bf16[2048,2,128]{0,2,1:T(8,128)(2,1)} %bitcast.189), kind=kOutput, calls=%fused_computation.12 | convolution fusion | flops 2172645376 | bytes 39862272 | tf_op jit(solution)/shard_map/nkgd,mkd->kgnm/dot_general | solution.py:45
  216.3 16.1 %fusion.3 = (f32[2,2048]{1,0:T(2,128)S(1)}, f32[2,2048,2048]{2,1,0:T(8,128)}) fusion(pred[2048,2048]{0,1:T(8,128)(4,1)S(1)} %copy-done.1, bf16[2048,2,128]{0,2,1:T(8,128)(2,1)} %bitcast.184, bf16[2048,2,128]{0,2,1:T(8,128)(2,1)} %bitcast.190), kind=kOutput, calls=%fused_computation.15 | convolution fusion | flops 2172645376 | bytes 39862272 | tf_op jit(solution)/shard_map/nkgd,mkd->kgnm/dot_general | solution.py:45
  232.4 16.7 %fusion.2 = (f32[2,2048]{1,0:T(2,128)S(1)}, f32[2,2048,2048]{2,1,0:T(8,128)}) fusion(pred[2048,2048]{0,1:T(8,128)(4,1)} %get-tuple-element.26, bf16[2048,2,128]{0,2,1:T(8,128)(2,1)} %bitcast.183, bf16[2048,2,128]{0,2,1:T(8,128)(2,1)} %bitcast.191), kind=kOutput, calls=%fused_computation.14 | convolution fusion | flops 2172645376 | bytes 39862272 | tf_op jit(solution)/shard_map/nkgd,mkd->kgnm/dot_general | solution.py:45
  249.0 0.0 copy-done.2
  249.0 16.0 %fusion.1 = (f32[2,2048]{1,0:T(2,128)S(1)}, f32[2,2048,2048]{2,1,0:T(8,128)}) fusion(pred[2048,2048]{0,1:T(8,128)(4,1)S(1)} %copy-done.2, bf16[2048,2,128]{0,2,1:T(8,128)(2,1)} %bitcast.182, bf16[2048,2,128]{0,2,1:T(8,128)(2,1)} %bitcast.192), kind=kOutput, calls=%fused_computation.13 | convolution fusion | flops 2172645376 | bytes 39862272 | tf_op jit(solution)/shard_map/nkgd,mkd->kgnm/dot_general | solution.py:45
  265.1 25.6 %fusion.4 = (f32[2,2048]{1,0:T(2,128)S(1)}, f32[2,2048]{1,0:T(2,128)S(1)}) fusion(f32[2,2048,2048]{2,1,0:T(8,128)} %get-tuple-element.35, f32[2,2048]{1,0:T(2,128)S(1)} %get-tuple-element.23, pred[2048,2048]{0,1:T(8,128)(4,1)} %get-tuple-element.24, f32[2,2048]{1,0:T(2,128)S(1)} %get-tuple-element.11, f32[2,2048,2048]{2,1,0:T(8,128)} %get-tuple-element.33, ...), kind=kLoop, calls=%fused_computation.16 | loop fusion | flops 83877888 | bytes 75563008 | tf_op jit(solution)/shard_map/reduce_sum | solution.py:50
  290.7 25.4 %fusion.8 = (f32[2,2048]{1,0:T(2,128)S(1)}, f32[2,2048]{1,0:T(2,128)S(1)}) fusion(f32[2,2048,2048]{2,1,0:T(8,128)} %get-tuple-element.31, f32[2,2048]{1,0:T(2,128)S(1)} %get-tuple-element.10, pred[2048,2048]{0,1:T(8,128)(4,1)} %get-tuple-element.26, f32[2,2048]{1,0:T(2,128)S(1)} %get-tuple-element.9, f32[2,2048,2048]{2,1,0:T(8,128)} %get-tuple-element.29, ...), kind=kLoop, calls=%fused_computation.20 | loop fusion | flops 83877888 | bytes 75563008 | tf_op jit(solution)/shard_map/reduce_sum | solution.py:50
  316.1 0.1 multiply_add_fusion
  316.2 18.7 %fusion.57 = f32[2,2048,128]{1,2,0:T(8,128)} fusion(bf16[2048,2,128]{0,2,1:T(8,128)(2,1)} %bitcast.181, f32[2,2048,2048]{2,1,0:T(8,128)} %get-tuple-element.35, f32[2,2048]{1,0:T(2,128)S(1)} %get-tuple-element.23, pred[2048,2048]{0,1:T(8,128)(4,1)} %get-tuple-element.24, f32[2,2048]{1,0:T(2,128)S(1)} %get-tuple-element.6, f32[2,2048]{1,0:T(2,128)S(1)} %get-tuple-element.22), kind=kOutput, calls=%fused_computation.55 | convolution fusion | flops 2190475264 | bytes 40943616 | tf_op jit(solution)/shard_map/kgnm,mkd->kgnd/dot_general | solution.py:51
  334.8 0.0 copy-done.5
  334.8 18.9 %fusion.51 = f32[2,2048,128]{1,2,0:T(8,128)} fusion(f32[2,2048,128]{1,2,0:T(8,128)} %fusion.57, bf16[2048,2,128]{0,2,1:T(8,128)(2,1)S(1)} %bitcast.180, f32[2,2048,2048]{2,1,0:T(8,128)} %get-tuple-element.33, f32[2,2048]{1,0:T(2,128)S(1)} %get-tuple-element.11, pred[2048,2048]{0,1:T(8,128)(4,1)} %get-tuple-element.25, f32[2,2048]{1,0:T(2,128)S(1)} %get-tuple-element.7), kind=kOutput, calls=%fused_computation.53 | convolution fusion | flops 2190475264 | bytes 43024384 | tf_op jit(solution)/shard_map/kgnm,mkd->kgnd/dot_general | solution.py:51
  353.7 18.6 %fusion.45 = f32[2,2048,128]{1,2,0:T(8,128)} fusion(f32[2,2048,128]{1,2,0:T(8,128)} %fusion.51, bf16[2048,2,128]{0,2,1:T(8,128)(2,1)S(1)} %bitcast.179, f32[2,2048,2048]{2,1,0:T(8,128)} %get-tuple-element.31, f32[2,2048]{1,0:T(2,128)S(1)} %get-tuple-element.10, pred[2048,2048]{0,1:T(8,128)(4,1)} %get-tuple-element.26, f32[2,2048]{1,0:T(2,128)S(1)} %get-tuple-element.8), kind=kOutput, calls=%fused_computation.51 | convolution fusion | flops 2190475264 | bytes 43024384 | tf_op jit(solution)/shard_map/kgnm,mkd->kgnd/dot_general | solution.py:51
  372.3 17.4 %divide_convert_fusion = bf16[2,2048,128]{1,2,0:T(8,128)(2,1)S(1)} fusion(f32[2,2048]{1,0:T(2,128)S(1)} %get-tuple-element.5, f32[2,2048,128]{1,2,0:T(8,128)} %fusion.45, bf16[2048,2,128]{0,2,1:T(8,128)(2,1)S(1)} %bitcast.178, f32[2,2048,2048]{2,1,0:T(8,128)} %get-tuple-element.29, f32[2,2048]{1,0:T(2,128)S(1)} %get-tuple-element.9, ...), kind=kOutput, calls=%fused_computation.62 | convolution fusion | flops 2190999552 | bytes 41975808 | tf_op jit(solution)/shard_map/kgnm,mkd->kgnd/dot_general | solution.py:51
  389.7 8.1 %fusion.102 = f32[2048,2048]{1,0:T(8,128)} fusion(bf16[2048,256]{0,1:T(8,128)(2,1)S(1)} %bitcast.186, bf16[256,2048]{1,0:T(8,128)(2,1)S(1)} %copy-done), kind=kOutput, calls=%fused_computation.130 | convolution fusion | flops 2147483648 | bytes 18874368 | tf_op jit(solution)/shard_map/dot_general | solution.py:54
  397.8 0.1 reduce-scatter.2.cloned.1.call-update
  397.9 0.6 copy-done.6
  398.5 0.1 copy.41
  398.7 0.1 eq.23
  398.8 0.1 broadcast_in_dim_reshape.4
  398.9 0.1 reshape.484
  399.1 1.2 reduce-window.6
  400.3 0.2 slice_reduce_fusion
  400.6 0.1 bitcast_bitcast_fusion
  400.7 4.5 gather_fusion.2
  405.3 81.8 %reduce-scatter.2.cloned.1.call-done = f32[256,2048]{1,0:T(8,128)} async-done(((f32[2048,2048]{1,0:T(8,128)}), f32[256,2048]{1,0:T(8,128)}) %reduce-scatter.2.cloned.1.call-update) | async-done | bytes 2097168 | tf_op jit(solution)/shard_map/reduce_scatter | solution.py:55
  487.1 0.0 copy-done.3
  487.1 1.9 add_convert_fusion.1
  489.0 3.3 gather_fusion
  492.3 2.4 broadcast_in_dim.120
  494.8 91.8 %scatter_fusion = bf16[32,32,2048]{2,1,0:T(8,128)(2,1)} fusion(bf16[32,32,2048]{2,1,0:T(8,128)(2,1)} %broadcast_in_dim.120, s32[512]{0:T(512)S(1)} %bitcast.173, bf16[512,2048]{1,0:T(8,128)(2,1)} %gather_fusion), kind=kCustom, calls=%fused_computation.3 | custom fusion | bytes 6295552 | tf_op jit(solution)/shard_map/scatter | solution.py:75
  586.6 57.2 %all_to_all.10 = bf16[32,32,2048]{2,1,0:T(8,128)(2,1)S(1)} all-to-all(bf16[32,32,2048]{2,1,0:T(8,128)(2,1)} %scatter_fusion), channel_id=1, replica_groups=mesh['dp'=1,'cp'=4,'tp'=8] {'cp','tp'}, dimensions={0} | all-to-all | bytes 8388608 | tf_op jit(solution)/shard_map/all_to_all | solution.py:76
  643.7 4.5 fusion.30
  648.3 0.0 copy-start.11
  648.3 5.4 multiply_convert_fusion
  653.7 6.1 fusion.34
  659.8 8.2 %all-to-all-start.1 = ((bf16[32,32,2048]{2,1,0:T(8,128)(2,1)}), bf16[32,32,2048]{2,1,0:T(8,128)(2,1)}, u32[]{:S(2)}, u32[]{:S(2)}) async-start(bf16[32,32,2048]{2,1,0:T(8,128)(2,1)} %bitcast.175), calls=%async_computation.2 | async-start | bytes 8388608 | tf_op jit(solution)/shard_map/all_to_all | solution.py:78
  667.9 0.1 copy.40
  668.1 52.7 %all-to-all-done.1 = bf16[32,32,2048]{2,1,0:T(8,128)(2,1)} async-done(((bf16[32,32,2048]{2,1,0:T(8,128)(2,1)}), bf16[32,32,2048]{2,1,0:T(8,128)(2,1)}, u32[]{:S(2)}, u32[]{:S(2)}) %all-to-all-start.1) | async-done | bytes 4194336 | tf_op jit(solution)/shard_map/all_to_all | solution.py:78
  720.8 13.0 %gather_fusion.1 = bf16[512,2048]{1,0:T(8,128)(2,1)} fusion(bf16[32,32,2048]{2,1,0:T(8,128)(2,1)} %all-to-all-done.1, s32[512]{0:T(512)S(1)} %bitcast.172), kind=kCustom, calls=%fused_computation.1 | custom fusion | bytes 4198400 | tf_op jit(solution)/shard_map/gather | solution.py:79
  733.8 5.4 reshape.488
  739.2 8.9 %multiply_reduce_fusion = f32[256,2048]{1,0:T(8,128)S(1)} fusion(f32[256,2,2048]{2,1,0:T(2,128)} %reshape.488, f32[256,2]{1,0:T(8,128)S(1)} %copy.40), kind=kLoop, calls=%fused_computation.46 | loop fusion | flops 1572864 | bytes 6293504 | tf_op jit(solution)/shard_map/reduce_sum | solution.py:80
  748.1 1.3 add_convert_fusion
  (39 shorter events, 0.2 us)
Async XLA Ops:
  6.5 383.2 %copy-start = (bf16[256,2048]{1,0:T(8,128)(2,1)S(1)}, bf16[256,2048]{1,0:T(8,128)(2,1)}, u32[]{:S(2)}) copy-start(bf16[256,2048]{1,0:T(8,128)(2,1)} %param.16) | copy-start | bytes 3145732
  6.6 50.2 %all-gather.4.cloned.1.call-start = ((), (), s32[]{:S(2)}) async-start(), calls=%async_computation.3 | async-start | bytes 9437184 | tf_op jit(solution)/shard_map/all_gather | solution.py:19
  7.3 55.6 %copy-start.12 = (bf16[2048,256]{1,0:T(8,128)(2,1)S(1)}, bf16[2048,256]{1,0:T(8,128)(2,1)}, u32[]{:S(2)}) copy-start(bf16[2048,256]{1,0:T(8,128)(2,1)} %param.14) | copy-start | bytes 3145732
  7.3 141.6 %all-gather.6.cloned.1.call-start = ((), (), s32[]{:S(2)}) async-start(), calls=%async_computation.5 | async-start | bytes 10485760 | tf_op jit(solution)/shard_map/all_gather | solution.py:28
  56.7 6.2 copy-start.8
  66.8 420.2 %reduce-scatter.2.cloned.1.call-start = ((), (), s32[]{:S(2)}) async-start(), calls=%async_computation.4 | async-start | bytes 18874368 | tf_op jit(solution)/shard_map/reduce_scatter | solution.py:55
  67.2 10.5 %copy-start.13 = (bf16[2048,256]{1,0:T(8,128)(2,1)S(1)}, bf16[2048,256]{1,0:T(8,128)(2,1)}, u32[]{:S(2)}) copy-start(bf16[2048,256]{1,0:T(8,128)(2,1)} %param.13) | copy-start | bytes 3145732
  199.6 16.7 %copy-start.1 = (pred[2048,2048]{0,1:T(8,128)(4,1)S(1)}, pred[2048,2048]{0,1:T(8,128)(4,1)}, u32[]{:S(2)}) copy-start(pred[2048,2048]{0,1:T(8,128)(4,1)} %get-tuple-element.27) | copy-start | bytes 12582916
  232.4 16.7 %copy-start.2 = (pred[2048,2048]{0,1:T(8,128)(4,1)S(1)}, pred[2048,2048]{0,1:T(8,128)(4,1)}, u32[]{:S(2)}) copy-start(pred[2048,2048]{0,1:T(8,128)(4,1)} %get-tuple-element.25) | copy-start | bytes 12582916
  316.2 18.7 %copy-start.5 = (bf16[1,2048,256]{1,2,0:T(8,128)(2,1)S(1)}, bf16[1,2048,256]{1,2,0:T(8,128)(2,1)}, u32[]{:S(2)}) copy-start(bf16[1,2048,256]{1,2,0:T(8,128)(2,1)} %copy.60) | copy-start | bytes 3145732
  353.7 18.6 %copy-start.4 = (bf16[1,2048,256]{1,2,0:T(8,128)(2,1)S(1)}, bf16[1,2048,256]{1,2,0:T(8,128)(2,1)}, u32[]{:S(2)}) copy-start(bf16[1,2048,256]{1,2,0:T(8,128)(2,1)} %copy.64) | copy-start | bytes 3145732
  397.8 0.7 copy-start.6
  397.8 89.2 %copy-start.3 = (bf16[256,2048]{1,0:T(8,128)(2,1)S(1)}, bf16[256,2048]{1,0:T(8,128)(2,1)}, u32[]{:S(2)}) copy-start(bf16[256,2048]{1,0:T(8,128)(2,1)} %param.10) | copy-start | bytes 3145732
  586.6 57.2 %copy-start.9 = (bf16[1,2048,1024]{2,1,0:T(8,128)(2,1)S(1)}, bf16[1,2048,1024]{2,1,0:T(8,128)(2,1)}, u32[]{:S(2)}) copy-start(bf16[1,2048,1024]{2,1,0:T(8,128)(2,1)} %param.18) | copy-start | bytes 12582916
  643.7 4.5 copy-start.10
  648.3 5.4 copy-start.11
  659.8 8.2 %copy-start.7 = (f32[256,2]{0,1:T(2,128)S(1)}, f32[256,2]{0,1:T(2,128)}, u32[]{:S(2)}) copy-start(f32[256,2]{0,1:T(2,128)} %param.12) | copy-start | bytes 6148
  659.8 61.0 %all-to-all-start.1 = ((bf16[32,32,2048]{2,1,0:T(8,128)(2,1)}), bf16[32,32,2048]{2,1,0:T(8,128)(2,1)}, u32[]{:S(2)}, u32[]{:S(2)}) async-start(bf16[32,32,2048]{2,1,0:T(8,128)(2,1)} %bitcast.175), calls=%async_computation.2 | async-start | bytes 8388608 | tf_op jit(solution)/shard_map/all_to_all | solution.py:78
Sparse Core Ops, SparseCore 0:
  9.0 47.7 all-gather.3
  66.9 81.9 all-gather.5
  398.0 88.9 reduce-scatter.1
where the time goes:
time: 768 us; the launch traced here: 756 us
  waiting for transfers between devices  249 us (32%)
  matrix products  178 us (23%)
  local copies, waits for them, and re-layouts  173 us (23%)
  other arithmetic  76.6 us (10%)
  blocking collectives  57.2 us (7%)
  between operations  13.7 us (2%)
  starting transfers between devices  8.58 us (1%)
    scatter x1, local copies, waits for them, and re-layouts, local(): send = jnp.zeros((ne, cap, hd), jnp.bfloat16).at[ea, slot].set(h[tok])  91.8 us
    reduce_scatter x1, waiting for transfers between devices, attention_residual(): att = lax.psum_scatter(part, 'tp', scatter_dimension=0, tiled=True)  81.8 us
    dot_general x4, matrix products, attention_residual(): jnp.einsum('kgnm,mkd->kgnd', w.astype(jnp.bfloat16), vj, preferred_elemen...  73.5 us
    dot_general x4, matrix products, attention_residual(): jnp.einsum('nkgd,mkd->kgnm', q4, kj, preferred_element_type=jnp.float32)  65.4 us
    all_gather x1, waiting for transfers between devices, attention_residual(): kvs = lax.all_gather(jnp.concatenate([k, v], axis=1), 'cp', axis=0)  64.5 us
    all_to_all x1, blocking collectives, local(): recv = lax.all_to_all(send, ('cp', 'tp'), 0, 0, tiled=True)  57.2 us
    all_to_all x1, waiting for transfers between devices, local(): lax.all_to_all(z.reshape(ne, cap, hd), ('cp', 'tp'), 0, 0, tiled=True)  52.7 us
    reduce_sum x2, other arithmetic, attention_residual(): l = l * c + jnp.sum(w, axis=-1)  51 us
  transfers between devices with their start and end apart: 4, of which 4 were waited for; matrix products, arithmetic and copies ran while one was open for 3% of the time, Pallas kernels for 0%

commit v1 on v0

v1 whole, which is shorter than its diff:
```python
import functools
import math

import jax
import jax.numpy as jnp
from jax import lax
from jax.experimental import pallas as pl
from jax.experimental.pallas import tpu as pltpu
from jax.sharding import PartitionSpec as P

HEAD = 128
MESH = pl.DeviceIdType.MESH
VMEM = pltpu.VMEM
DMA = pltpu.SemaphoreType.DMA
BF16 = jnp.bfloat16
F32 = jnp.float32


def spec(space):
    return pl.BlockSpec(memory_space=space)


def remote(src, dst, ssem, rsem, dev):
    return pltpu.make_async_remote_copy(src_ref=src, dst_ref=dst, send_sem=ssem, recv_sem=rsem, device_id=dev, device_id_type=MESH)


def barrier_with(devs):
    b = pltpu.get_barrier_semaphore()
    for d in devs:
        pl.semaphore_signal(b, inc=1, device_id=d, device_id_type=MESH)
    pl.semaphore_wait(b, len(devs))


def place(c, chip, core, cp):
    high = chip // 2
    seg = c * (1 - high) + (2 * cp - 1 - c) * high
    return seg * 4 + (chip % 2) * 2 + core


def qkv_kernel(cp, nx, x_ref, wq_ref, wk_ref, wv_ref, kvq, wsib, xb, stage, wss, wrs, xss, xrs, ass, ars, rss, rrs, ls):
    c = lax.axis_index('cp')
    t = lax.axis_index('tp')
    i, k = t // 2, t % 2
    T = x_ref.shape[0]
    half = T // 2
    sib = {'cp': c, 'tp': i * 2 + 1 - k}
    right = {'cp': c, 'tp': ((i + 1) % nx) * 2 + k}
    left = {'cp': c, 'tp': ((i + nx - 1) % nx) * 2 + k}
    peer = [{'cp': (c + d) % cp, 'tp': t} for d in range(cp)]
    barrier_with([sib, right, left] + peer[1:])
    lo, hi = pl.ds(0, half), pl.ds(half, half)
    full = pl.ds(0, T)

    def xcopy(n, src, slot, rows, dev):
        return remote(src.at[rows], xb.at[slot, rows], xss.at[n], xrs.at[n], dev)

    sends = [
        xcopy(0, x_ref, 0, lo, right), xcopy(1, x_ref, 1, hi, left),
        xcopy(2, x_ref, 0, hi, right), xcopy(3, x_ref, 1, lo, left),
    ]
    own_w = [wq_ref, wk_ref, wv_ref]
    wsend = [remote(own_w[n], wsib.at[n], wss.at[n], wrs.at[n], sib) for n in range(3)]
    for s in (sends[0], sends[1], *wsend, sends[2], sends[3]):
        s.start()

    pend = list(sends) + wsend
    arrive = []

    units = [(0, full), (nx - 1, lo), (1, hi), (nx - 1, hi), (1, lo), (2, lo), (2, hi)]

    def compute(u, src, rows):
        xv = src[rows, :]
        for w in range(2):
            if u == 0 and w == 1:
                for s in wsend:
                    s.wait_recv()
            for n in range(3):
                wref = own_w[n] if w == 0 else wsib.at[n]
                r = jnp.dot(xv, wref[...], preferred_element_type=F32).astype(BF16)
                kk = k if w == 0 else 1 - k
                for m in range(2):
                    stage[u, 2 * kk + m, n, rows, :] = r[:, m * HEAD:(m + 1) * HEAD]

    def block_of(u, d):
        dj, _ = units[u]
        return place((c + cp - d) % cp, (i + dj) % nx, k, cp)

    def send(u):
        rows = units[u][1]
        b = block_of(u, 0)
        for d in range(1, cp):
            cps = remote(stage.at[u, (c + d) % cp, :, rows], kvq.at[b, :, rows], ass.at[u, d], ars.at[u, d], peer[d])
            cps.start()
            pend.append(cps)
        lc = pltpu.make_async_copy(stage.at[u, c, :, rows], kvq.at[b, :, rows], ls.at[u])
        lc.start()
        locs.append(lc)
        relay(u, 0, stage.at[u, c, pl.ds(1, 2), rows])

    def relay(u, d, src):
        rows = units[u][1]
        b = block_of(u, d)
        cps = remote(src, kvq.at[b, pl.ds(1, 2), rows], rss.at[u, d], rrs.at[u, d], sib)
        cps.start()
        pend.append(cps)
        arrive.append((u, d))

    def pass_on(u):
        rows = units[u][1]
        for d in range(1, cp):
            b = block_of(u, d)
            remote(stage.at[u, 0, :, rows], kvq.at[b, :, rows], ass.at[u, d], ars.at[u, d], peer[d]).wait_recv()
            relay(u, d, kvq.at[b, pl.ds(1, 2), rows])

    locs = []
    compute(0, x_ref, full)
    send(0)
    sends[0].wait_recv()
    f = xcopy(4, xb.at[0], 2, lo, right)
    f.start()
    g = xcopy(5, xb.at[1], 2, hi, left)
    sends[1].wait_recv()
    g.start()
    pend += [f, g]
    compute(1, xb.at[0], lo)
    send(1)
    compute(2, xb.at[1], hi)
    send(2)
    pass_on(0)
    sends[2].wait_recv()
    compute(3, xb.at[0], hi)
    send(3)
    sends[3].wait_recv()
    compute(4, xb.at[1], lo)
    send(4)
    pass_on(1)
    pass_on(2)
    f.wait_recv()
    compute(5, xb.at[2], lo)
    send(5)
    g.wait_recv()
    compute(6, xb.at[2], hi)
    send(6)
    for u in range(3, 7):
        pass_on(u)
    for u, d in arrive:
        rows = units[u][1]
        b = block_of(u, d) + 1 - 2 * k
        remote(stage.at[u, 0, pl.ds(1, 2), rows], kvq.at[b, pl.ds(1, 2), rows], rss.at[u, d], rrs.at[u, d], sib).wait_recv()
    for lc in locs:
        lc.wait()
    for s in pend:
        s.wait_send()


def attn_kernel(cp, nx, kvq, wo_ref, x_ref, h_ref, vt, wof, ostage, obuf, wss, wrs, oss, ors, ls):
    c = lax.axis_index('cp')
    t = lax.axis_index('tp')
    i, k = t // 2, t % 2
    T, H = x_ref.shape
    R = wo_ref.shape[0]
    nch = kvq.shape[0] // 2
    sib = {'cp': c, 'tp': i * 2 + 1 - k}
    ri, li, oi = (i + 1) % nx, (i + nx - 1) % nx, (i + 2) % nx
    right = {'cp': c, 'tp': ri * 2 + k}
    left = {'cp': c, 'tp': li * 2 + k}
    offs = [(di, dc) for di in range(nx) for dc in range(cp)]

    def dev(di, dc):
        return {'cp': (c + dc) % cp, 'tp': ((i + di) % nx) * 2 + k}

    barrier_with([sib] + [dev(di, dc) for di, dc in offs[1:]])
    half = R // 2
    lo, hi, full = pl.ds(0, half), pl.ds(half, half), pl.ds(0, R)
    own = t

    def wcopy(n, src, chip, core, rows, to):
        return remote(src, wof.at[chip * 2 + core, rows], wss.at[n], wrs.at[n], to)

    w0 = wcopy(0, wo_ref.at[lo], i, k, lo, right)
    w1 = wcopy(1, wo_ref.at[hi], i, k, hi, left)
    w2 = wcopy(2, wo_ref.at[hi], i, k, hi, right)
    w3 = wcopy(3, wo_ref.at[lo], i, k, lo, left)
    w6 = wcopy(6, wo_ref, i, k, full, sib)
    for w in (w0, w1, w2, w3, w6):
        w.start()
    wl = pltpu.make_async_copy(wo_ref, wof.at[t], ls.at[0])
    wl.start()
    w4 = wcopy(4, wof.at[li * 2 + k, lo], li, k, lo, right)
    w5 = wcopy(5, wof.at[ri * 2 + k, hi], ri, k, hi, left)
    w7 = wcopy(7, wof.at[li * 2 + k], li, k, full, sib)
    w8 = wcopy(8, wof.at[ri * 2 + k], ri, k, full, sib)
    w9 = wcopy(9, wof.at[oi * 2 + k], oi, k, full, sib)

    @pl.loop(0, nch)
    def _(m):
        v = kvq[pl.ds(2 * m, 2), 2].reshape(2 * T, HEAD)
        vt[m] = v.astype(F32).T.astype(BF16)

    scale = HEAD ** -0.5 * math.log2(math.e)

    def step(q, m, mask, carry):
        mo, l, acc = carry
        kb = kvq[pl.ds(2 * m, 2), 1].reshape(2 * T, HEAD)
        s = lax.dot_general(kb, q, (((1,), (1,)), ((), ())), preferred_element_type=F32)
        if mask is not None:
            s = jnp.where(mask, s, -jnp.inf)
        mn = jnp.maximum(mo, jnp.max(s, axis=0, keepdims=True))
        w = jnp.exp2((s - mn) * scale)
        a = jnp.exp2((mo - mn) * scale)
        l = l * a + jnp.sum(w, axis=0, keepdims=True)
        acc = acc * a + jnp.dot(vt[m], w.astype(BF16), preferred_element_type=F32)
        return mn, l, acc

    rows_i = lax.broadcasted_iota(jnp.int32, (2 * T, T), 0)
    cols_i = lax.broadcasted_iota(jnp.int32, (2 * T, T), 1)
    order = offs[1:] + offs[:1]

    def attend(n):
        di, dc = n // cp, n % cp
        pb = place((c + dc) % cp, (i + di) % nx, k, cp)
        q = kvq[pb, 0]
        m = pb // 2
        carry = (jnp.full((1, T), -jnp.inf, F32), jnp.zeros((1, T), F32), jnp.zeros((HEAD, T), F32))
        carry = lax.fori_loop(0, m, lambda j, cr: step(q, j, None, cr), carry)
        mo, l, acc = step(q, m, rows_i <= cols_i + k * T, carry)
        ostage[n] = (acc / l).T.astype(BF16)

    head = i * cp + c
    col = pl.ds((c % 2) * HEAD, HEAD)

    def osend(n, to):
        return remote(ostage.at[n], obuf.at[i * 2 + c // 2, :, col], oss.at[n], ors.at[n], to)

    nall = nx * cp

    def run(a, b):
        @pl.loop(a, b)
        def _(n):
            attend(n)
            osend(n, {'cp': (c + n % cp) % cp, 'tp': ((i + n // cp) % nx) * 2 + k}).start()

    run(1, 6)
    w0.wait_recv()
    w4.start()
    w1.wait_recv()
    w5.start()
    run(6, 11)
    w2.wait_recv()
    w7.start()
    w3.wait_recv()
    w8.start()
    run(11, nall)
    attend(0)
    lo_c = pltpu.make_async_copy(ostage.at[0], obuf.at[i * 2 + c // 2, :, col], ls.at[1])
    lo_c.start()
    w4.wait_recv()
    w5.wait_recv()
    w9.start()
    wl.wait()
    for w in (w6, w7, w8, w9):
        w.wait_recv()
    lo_c.wait()

    @pl.loop(1, nall)
    def _(n):
        osend(n, {'cp': (c + n % cp) % cp, 'tp': ((i + n // cp) % nx) * 2 + k}).wait_recv()

    nt = wof.shape[0]
    cw = min(512, H)
    for j in range(H // cw):
        cs = slice(j * cw, (j + 1) * cw)
        a = jnp.dot(obuf[0], wof[0, :, cs], preferred_element_type=F32)
        for tt in range(1, nt):
            a += jnp.dot(obuf[tt], wof[tt, :, cs], preferred_element_type=F32)
        h_ref[:, cs] = (x_ref[:, cs].astype(F32) + a).astype(BF16)

    for w in (w0, w1, w2, w3, w4, w5, w6, w7, w8, w9):
        w.wait_send()

    @pl.loop(1, nall)
    def _(n):
        osend(n, {'cp': (c + n % cp) % cp, 'tp': ((i + n // cp) % nx) * 2 + k}).wait_send()


def moe_kernel(cp, tp, cap, h_ref, p_ref, g0_ref, g1_ref, gates_ref, wg_hbm, wu_hbm, wd_hbm, y_ref,
               sendb, recvb, zb, back, wg, wu, wd, acc0, acc1, wsem, dss, drs, bss, brs):
    c = lax.axis_index('cp')
    t = lax.axis_index('tp')
    ne = cp * tp
    T, H = h_ref.shape
    grp = 4
    ng = ne // grp
    wc = [pltpu.make_async_copy(a.at[0], b, wsem.at[n]) for n, (a, b) in enumerate(((wg_hbm, wg), (wu_hbm, wu), (wd_hbm, wd)))]
    for w in wc:
        w.start()

    def fwd(d):
        return {'cp': (c + d // tp) % cp, 'tp': (t + d % tp) % tp}

    def bwd(d):
        return {'cp': (c + cp - d // tp) % cp, 'tp': (t + tp - d % tp) % tp}

    b = pltpu.get_barrier_semaphore()

    @pl.loop(1, ne)
    def _(d):
        pl.semaphore_signal(b, inc=1, device_id=fwd(d), device_id_type=MESH)

    def pack(g):
        rows = p_ref[pl.ds(g * grp * cap, grp * cap), :]
        r = jnp.dot(rows, h_ref[...], preferred_element_type=F32).astype(BF16)
        sendb[pl.ds(g * grp, grp)] = r.reshape(grp, cap, H)

    def disp(d):
        return remote(sendb.at[d], recvb.at[d], dss.at[d], drs.at[d], fwd(d))

    def ret(d):
        return remote(zb.at[d], back.at[d], bss.at[d], brs.at[d], bwd(d))

    pack(0)
    recvb[0] = sendb[0]
    pl.semaphore_wait(b, ne - 1)
    for d in range(1, grp):
        disp(d).start()

    @pl.loop(1, ng)
    def _(g):
        pack(g)
        for j in range(grp):
            disp(g * grp + j).start()

    for w in wc:
        w.wait()

    def ffn(g):
        rows = recvb[pl.ds(g * grp, grp)].reshape(grp * cap, H)
        gg = jnp.dot(rows, wg[...], preferred_element_type=F32)
        uu = jnp.dot(rows, wu[...], preferred_element_type=F32)
        act = (gg * jax.nn.sigmoid(gg) * uu).astype(BF16)
        z = jnp.dot(act, wd[...], preferred_element_type=F32).astype(BF16)
        zb[pl.ds(g * grp, grp)] = z.reshape(grp, cap, H)

    def combine(g):
        zz = back[pl.ds(g * grp, grp)].reshape(grp * cap, H)
        cols = pl.ds(pl.multiple_of(g * grp * cap, grp * cap), grp * cap)
        return (jnp.dot(g0_ref[:, cols], zz, preferred_element_type=F32),
                jnp.dot(g1_ref[:, cols], zz, preferred_element_type=F32))

    for d in range(1, grp):
        disp(d).wait_recv()
    ffn(0)
    back[0] = zb[0]
    for d in range(1, grp):
        ret(d).start()

    @pl.loop(1, ng)
    def _(g):
        for j in range(grp):
            disp(g * grp + j).wait_recv()
        ffn(g)
        for j in range(grp):
            ret(g * grp + j).start()

    for d in range(1, grp):
        ret(d).wait_recv()
    a, bb = combine(0)
    acc0[...] = a
    acc1[...] = bb

    @pl.loop(1, ng)
    def _(g):
        for j in range(grp):
            ret(g * grp + j).wait_recv()
        a, bb = combine(g)
        acc0[...] += a
        acc1[...] += bb

    y_ref[...] = (h_ref[...].astype(F32) + (gates_ref[:, 0:1] * acc0[...] + gates_ref[:, 1:2] * acc1[...])).astype(BF16)

    @pl.loop(1, ne)
    def _(d):
        disp(d).wait_send()
        ret(d).wait_send()


def params(cid):
    return pltpu.CompilerParams(collective_id=cid, has_side_effects=True, vmem_limit_bytes=60 * 1024 * 1024)


def attention(x, wq, wk, wv, wo, cp, tp):
    T, H = x.shape
    nx = tp // 2
    nb = cp * tp
    W = wq.shape[1]
    kvq = pl.pallas_call(
        functools.partial(qkv_kernel, cp, nx),
        out_shape=jax.ShapeDtypeStruct((nb, 3, T, HEAD), BF16),
        in_specs=[spec(VMEM)] * 4,
        out_specs=spec(VMEM),
        scratch_shapes=[
            VMEM((3, H, W), BF16), VMEM((3, T, H), BF16), VMEM((7, 4, 3, T, HEAD), BF16),
            DMA((3,)), DMA((3,)), DMA((6,)), DMA((6,)),
            DMA((7, cp)), DMA((7, cp)), DMA((7, cp)), DMA((7, cp)), DMA((7,)),
        ],
        compiler_params=params(0),
        name='qkv',
    )(x, wq, wk, wv)
    h = pl.pallas_call(
        functools.partial(attn_kernel, cp, nx),
        out_shape=jax.ShapeDtypeStruct((T, H), BF16),
        in_specs=[spec(VMEM)] * 3,
        out_specs=spec(VMEM),
        scratch_shapes=[
            VMEM((nb // 2, HEAD, 2 * T), BF16), VMEM((tp, wo.shape[0], H), BF16),
            VMEM((nx * cp, T, HEAD), BF16), VMEM((tp, T, 2 * HEAD), BF16),
            DMA((10,)), DMA((10,)), DMA((nx * cp,)), DMA((nx * cp,)), DMA((2,)),
        ],
        compiler_params=params(1),
        name='attn',
    )(kvq, wo, x)
    return h


def routing(idx, cp, tp, cap):
    ne = cp * tp
    T, kk = idx.shape
    c = lax.axis_index('cp')
    t = lax.axis_index('tp')
    rel = ((idx // tp - c + cp) % cp) * tp + (idx % tp - t + tp) % tp
    ea = rel.reshape(-1)
    onehot = (ea[:, None] == jnp.arange(ne)[None, :]).astype(jnp.int32)
    rank = jnp.cumsum(onehot, axis=0)
    slot = jnp.sum(onehot * rank, axis=1) - 1
    pos = (ea * cap + slot).reshape(T, kk)
    cols = jnp.arange(ne * cap, dtype=jnp.int32)
    g0 = pos[:, 0:1] == cols[None, :]
    g1 = pos[:, 1:2] == cols[None, :]
    p = (pos[:, 0][None, :] == cols[:, None]) | (pos[:, 1][None, :] == cols[:, None])
    return p.astype(BF16), g0.astype(BF16), g1.astype(BF16)


def experts(h, idx, gates, w1g, w1u, w2, cp, tp):
    T, H = h.shape
    F = w1g.shape[2]
    ne = cp * tp
    cap = 4 * T // ne
    p, g0, g1 = routing(idx, cp, tp, cap)
    return pl.pallas_call(
        functools.partial(moe_kernel, cp, tp, cap),
        out_shape=jax.ShapeDtypeStruct((T, H), BF16),
        in_specs=[spec(VMEM)] * 5 + [spec(pl.ANY)] * 3,
        out_specs=spec(VMEM),
        scratch_shapes=[VMEM((ne, cap, H), BF16)] * 4 + [
            VMEM((H, F), BF16), VMEM((H, F), BF16), VMEM((F, H), BF16), VMEM((T, H), F32), VMEM((T, H), F32),
            DMA((3,)), DMA((ne,)), DMA((ne,)), DMA((ne,)), DMA((ne,)),
        ],
        compiler_params=params(2),
        name='moe',
    )(h, p, g0, g1, gates, w1g, w1u, w2)


def solution(mesh):
    cp = mesh.shape['cp']
    tp = mesh.shape['tp']
    rows_spec = P(('dp', 'cp', 'tp'), None)
    exp_spec = P(('cp', 'tp'), None, None)

    def local(x, idx, gates, wq, wk, wv, wo, w1g, w1u, w2):
        h = attention(x, wq, wk, wv, wo, cp, tp)
        return experts(h, idx, gates, w1g, w1u, w2, cp, tp)

    return jax.shard_map(local, mesh=mesh, in_specs=(rows_spec, rows_spec, rows_spec, P(None, 'tp'), P(None, 'tp'), P(None, 'tp'), P('tp', None), exp_spec, exp_spec, exp_spec), out_specs=rows_spec, check_vma=False)
```

time: 768 us -> 306 us (0.40)
  Pallas kernels: 0 us -> 292 us
  waiting for transfers between devices: 249 us -> 0 us
  matrix products: 178 us -> 0 us
  local copies, waits for them, and re-layouts: 173 us -> 4.28 us
  other arithmetic: 76.6 us -> 3.87 us
  blocking collectives: 57.2 us -> 0 us
  between operations: 13.7 us -> 0.12 us
  starting transfers between devices: 8.58 us -> 0 us
    pallas_call x0 -> x3, Pallas kernels: none -> 292 us  [the longest x1 144 us: experts(): pl.pallas_call(functools.partial(moe_kernel, cp, tp, cap), out_shape=jax....]
    dot_general x15 -> x0, matrix products: 178 us -> none  [the longest x4 73.5 us: attention_residual(): jnp.einsum('kgnm,mkd->kgnd', w.astype(jnp.bfloat16), vj, preferred_elemen...]
    all_gather x2 -> x0, waiting for transfers between devices: 114 us -> none  [the longest x1 64.5 us: attention_residual(): kvs = lax.all_gather(jnp.concatenate([k, v], axis=1), 'cp', axis=0)]
    scatter x1 -> x0, local copies, waits for them, and re-layouts: 91.8 us -> none  [local(): send = jnp.zeros((ne, cap, hd), jnp.bfloat16).at[ea, slot].set(h[tok])]
    reduce_scatter x1 -> x0, waiting for transfers between devices: 81.8 us -> none  [attention_residual(): att = lax.psum_scatter(part, 'tp', scatter_dimension=0, tiled=True)]
    reduce_sum x3 -> x1, other arithmetic: 59.9 us -> 0.11 us  [routing(): slot = jnp.sum(onehot * rank, axis=1) - 1]
    all_to_all x1 -> x0, blocking collectives: 57.2 us -> none  [local(): recv = lax.all_to_all(send, ('cp', 'tp'), 0, 0, tiled=True)]
    all_to_all x1 -> x0, waiting for transfers between devices: 52.7 us -> none  [local(): lax.all_to_all(z.reshape(ne, cap, hd), ('cp', 'tp'), 0, 0, tiled=True)]
  transfers between devices with their start and end apart: 4 -> 0, of which waited for: 4 -> 0; matrix products, arithmetic and copies ran while one was open for 3% -> 0% of each run, Pallas kernels for 0% -> 0%
where the time goes in v1:
time: 306 us; the launch traced here: 300 us
  Pallas kernels  292 us (95%)
  local copies, waits for them, and re-layouts  4.28 us (1%)
  other arithmetic  3.87 us (1%)
    pallas_call x1, Pallas kernels, experts(): pl.pallas_call(functools.partial(moe_kernel, cp, tp, cap), out_shape=jax....  144 us
    pallas_call x1, Pallas kernels, attention(): pl.pallas_call(functools.partial(attn_kernel, cp, nx), out_shape=jax.Shap...  92.3 us
    pallas_call x1, Pallas kernels, attention(): pl.pallas_call(functools.partial(qkv_kernel, cp, nx), out_shape=jax.Shape...  55.8 us

profile of v1, /device:TPU:111, one launch (start us, length us, event | category | flops | bytes accessed | tf_op | source)
XLA Modules:
  0.0 299.9 jit_solution(8217678480478575851)
XLA Ops:
  0.0 55.8 %qkv.1.kvq = bf16[32,3,256,128]{3,2,1,0:T(8,128)(2,1)} custom-call(bf16[256,2048]{1,0:T(8,128)(2,1)} %x_ref.3, bf16[2048,256]{1,0:T(8,128)(2,1)} %wq_ref.1, bf16[2048,256]{1,0:T(8,128)(2,1)} %wk_ref.1, bf16[2048,256]{1,0:T(8,128)(2,1)} %wv_ref.1), custom_call_target="tpu_custom_call" | custom-call | tf_op jit(solution)/shard_map/qkv/pallas_call | solution.py:396
  55.8 0.0 copy-start
  55.8 0.0 copy-start.1
  55.8 92.3 %attn.1.h_ref = bf16[256,2048]{1,0:T(8,128)(2,1)} custom-call(bf16[32,3,256,128]{3,2,1,0:T(8,128)(2,1)} %qkv.1.kvq, bf16[256,2048]{1,0:T(8,128)(2,1)} %wo_ref.1, bf16[256,2048]{1,0:T(8,128)(2,1)} %x_ref.3), custom_call_target="tpu_custom_call" | custom-call | tf_op jit(solution)/shard_map/attn/pallas_call | solution.py:409
  148.1 0.0 copy-done
  148.1 0.2 copy.26
  148.3 0.1 copy.21
  148.5 0.2 fusion.8
  148.7 0.1 eq.85
  148.9 0.1 eq.89
  149.0 1.2 reduce-window.6
  150.2 0.2 slice_reduce_fusion.2
  150.5 0.1 fusion.14
  150.6 0.1 sub.30
  150.7 0.2 slice_reduce_fusion.1
  151.0 1.0 fusion.1.p_ref
  152.0 1.3 fusion.2
  153.2 0.0 copy-done.1
  153.2 0.8 copy.29.gates_ref
  154.0 143.6 %moe.1 = bf16[256,2048]{1,0:T(8,128)(2,1)} custom-call(bf16[256,2048]{1,0:T(8,128)(2,1)} %attn.1.h_ref, bf16[1024,256]{1,0:T(8,128)(2,1)} %fusion.1.p_ref, bf16[256,1024]{1,0:T(8,128)(2,1)} %get-tuple-element.7.g0_ref, bf16[256,1024]{1,0:T(8,128)(2,1)} %get-tuple-element.8.g1_ref, f32[256,2]{1,0:T(8,128)} %copy.29.gates_ref, bf16[1,2048,1024]{2,1,0:T(8,128)(2,1)} %wg_hbm.1, ...), custom_call_target="tpu_custom_call" | custom-call | tf_op jit(solution)/shard_map/moe/pallas_call | solution.py:449
  297.6 2.3 copy.36
  (6 shorter events, 0.1 us)
Async XLA Ops:
  55.8 92.3 %copy-start = (s32[256,2]{0,1:T(2,128)S(1)}, s32[256,2]{0,1:T(2,128)}, u32[]{:S(2)}) copy-start(s32[256,2]{0,1:T(2,128)} %param.11) | copy-start | bytes 6148
  55.8 97.4 %copy-start.1 = (f32[256,2]{0,1:T(2,128)S(1)}, f32[256,2]{0,1:T(2,128)}, u32[]{:S(2)}) copy-start(f32[256,2]{0,1:T(2,128)} %param.12) | copy-start | bytes 6148

commit v2 on v1

--- a/solution.py
+++ b/solution.py
@@ -153,7 +153,7 @@
         s.wait_send()
 
 
-def attn_kernel(cp, nx, kvq, wo_ref, x_ref, h_ref, vt, wof, ostage, obuf, wss, wrs, oss, ors, ls):
+def attn_kernel(cp, nx, kvq, wo_ref, x_ref, h_ref, vt, wof, ostage, obuf, sa, sb, acc, wss, wrs, oss, ors, ls):
     c = lax.axis_index('cp')
     t = lax.axis_index('tp')
     i, k = t // 2, t % 2
@@ -172,8 +172,6 @@
     barrier_with([sib] + [dev(di, dc) for di, dc in offs[1:]])
     half = R // 2
     lo, hi, full = pl.ds(0, half), pl.ds(half, half), pl.ds(0, R)
-    own = t
-
     def wcopy(n, src, chip, core, rows, to):
         return remote(src, wof.at[chip * 2 + core, rows], wss.at[n], wrs.at[n], to)
 
@@ -198,61 +196,83 @@
         vt[m] = v.astype(F32).T.astype(BF16)
 
     scale = HEAD ** -0.5 * math.log2(math.e)
-
-    def step(q, m, mask, carry):
-        mo, l, acc = carry
+    par = i % 2
+    col_i = lax.broadcasted_iota(jnp.int32, (1, 2 * T), 1)
+    qpos = col_i % T + k * T + 2 * T * jnp.where(col_i < T, par, 1 - par)
+    row_i = lax.broadcasted_iota(jnp.int32, (2 * T, 2 * T), 0)
+
+    def scores(q, m, buf):
         kb = kvq[pl.ds(2 * m, 2), 1].reshape(2 * T, HEAD)
-        s = lax.dot_general(kb, q, (((1,), (1,)), ((), ())), preferred_element_type=F32)
-        if mask is not None:
-            s = jnp.where(mask, s, -jnp.inf)
+        buf[...] = lax.dot_general(kb, q, (((1,), (1,)), ((), ())), preferred_element_type=F32)
+
+    def absorb(buf, m, part, ml):
+        mo, l = ml
+        s = buf[...]
+        if part is not None:
+            s = jnp.where(row_i + 2 * T * part <= qpos, s, -jnp.inf)
         mn = jnp.maximum(mo, jnp.max(s, axis=0, keepdims=True))
         w = jnp.exp2((s - mn) * scale)
         a = jnp.exp2((mo - mn) * scale)
         l = l * a + jnp.sum(w, axis=0, keepdims=True)
-        acc = acc * a + jnp.dot(vt[m], w.astype(BF16), preferred_element_type=F32)
-        return mn, l, acc
-
-    rows_i = lax.broadcasted_iota(jnp.int32, (2 * T, T), 0)
-    cols_i = lax.broadcasted_iota(jnp.int32, (2 * T, T), 1)
-    order = offs[1:] + offs[:1]
+        acc[...] = acc[...] * a + jnp.dot(vt[m], w.astype(BF16), preferred_element_type=F32)
+        return mn, l
 
     def attend(n):
-        di, dc = n // cp, n % cp
-        pb = place((c + dc) % cp, (i + di) % nx, k, cp)
-        q = kvq[pb, 0]
-        m = pb // 2
-        carry = (jnp.full((1, T), -jnp.inf, F32), jnp.zeros((1, T), F32), jnp.zeros((HEAD, T), F32))
-        carry = lax.fori_loop(0, m, lambda j, cr: step(q, j, None, cr), carry)
-        mo, l, acc = step(q, m, rows_i <= cols_i + k * T, carry)
-        ostage[n] = (acc / l).T.astype(BF16)
-
-    head = i * cp + c
+        cc = (c + n % cp) % cp
+        high = (i // 2 + n // cp) % 2
+        pb0 = place(cc, 2 * high + par, k, cp)
+        pb1 = place(cc, 2 * high + 1 - par, k, cp)
+        q = jnp.concatenate([kvq[pb0, 0], kvq[pb1, 0]], axis=0)
+        p = pb0 // 4
+        acc[...] = jnp.zeros_like(acc)
+        scores(q, 0, sa)
+
+        def body(j, ml):
+            scores(q, 2 * j + 1, sb)
+            ml = absorb(sa, 2 * j, None, ml)
+            scores(q, 2 * j + 2, sa)
+            return absorb(sb, 2 * j + 1, None, ml)
+
+        ml = (jnp.full((1, 2 * T), -jnp.inf, F32), jnp.zeros((1, 2 * T), F32))
+        ml = lax.fori_loop(0, p, body, ml)
+        scores(q, 2 * p + 1, sb)
+        ml = absorb(sa, 2 * p, 0, ml)
+        _, l = absorb(sb, 2 * p + 1, 1, ml)
+        o = (acc[...] / l).T.astype(BF16)
+        ostage[n, 0] = o[:T]
+        ostage[n, 1] = o[T:]
+
     col = pl.ds((c % 2) * HEAD, HEAD)
-
-    def osend(n, to):
-        return remote(ostage.at[n], obuf.at[i * 2 + c // 2, :, col], oss.at[n], ors.at[n], to)
-
-    nall = nx * cp
+    npair = 2 * cp
+
+    def owner(n, e, sign):
+        chip = 2 * ((i // 2 + n // cp) % 2) + (par + e) % 2
+        return {'cp': (c + sign * (n % cp) + cp) % cp, 'tp': chip * 2 + k}
+
+    def osend(n, e):
+        return remote(ostage.at[n, e], obuf.at[i * 2 + c // 2, :, col], oss.at[n, e], ors.at[n, e], owner(n, e, 1))
 
     def run(a, b):
         @pl.loop(a, b)
         def _(n):
             attend(n)
-            osend(n, {'cp': (c + n % cp) % cp, 'tp': ((i + n // cp) % nx) * 2 + k}).start()
-
-    run(1, 6)
+            osend(n, 0).start()
+            osend(n, 1).start()
+
+    run(1, 3)
     w0.wait_recv()
     w4.start()
     w1.wait_recv()
     w5.start()
-    run(6, 11)
+    run(3, 5)
     w2.wait_recv()
     w7.start()
     w3.wait_recv()
     w8.start()
-    run(11, nall)
+    run(5, npair)
     attend(0)
-    lo_c = pltpu.make_async_copy(ostage.at[0], obuf.at[i * 2 + c // 2, :, col], ls.at[1])
+    osend(0, 1).start()
+    lo_c = pltpu.make_async_copy(ostage.at[0, 0], obuf.at[i * 2 + c // 2, :, col], ls.at[1])
     lo_c.start()
     w4.wait_recv()
     w5.wait_recv()
@@ -261,10 +281,12 @@
     for w in (w6, w7, w8, w9):
         w.wait_recv()
     lo_c.wait()
-
-    @pl.loop(1, nall)
+    osend(0, 1).wait_recv()
+
+    @pl.loop(1, npair)
     def _(n):
-        osend(n, {'cp': (c + n % cp) % cp, 'tp': ((i + n // cp) % nx) * 2 + k}).wait_recv()
+        osend(n, 0).wait_recv()
+        osend(n, 1).wait_recv()
 
     nt = wof.shape[0]
     cw = min(512, H)
@@ -278,9 +300,12 @@
     for w in (w0, w1, w2, w3, w4, w5, w6, w7, w8, w9):
         w.wait_send()
 
-    @pl.loop(1, nall)
+    osend(0, 1).wait_send()
+
+    @pl.loop(1, npair)
     def _(n):
-        osend(n, {'cp': (c + n % cp) % cp, 'tp': ((i + n // cp) % nx) * 2 + k}).wait_send()
+        osend(n, 0).wait_send()
+        osend(n, 1).wait_send()
 
 
 def moe_kernel(cp, tp, cap, h_ref, p_ref, g0_ref, g1_ref, gates_ref, wg_hbm, wu_hbm, wd_hbm, y_ref,
@@ -295,11 +320,20 @@
     for w in wc:
         w.start()
 
+    nx = tp // 2
+    i, k = t // 2, t % 2
+
+    def offset(d):
+        w = d // 2
+        return w % cp, (w + w // cp) % nx, d % 2
+
     def fwd(d):
-        return {'cp': (c + d // tp) % cp, 'tp': (t + d % tp) % tp}
+        dc, di, dk = offset(d)
+        return {'cp': (c + dc) % cp, 'tp': ((i + di) % nx) * 2 + (k + dk) % 2}
 
     def bwd(d):
-        return {'cp': (c + cp - d // tp) % cp, 'tp': (t + tp - d % tp) % tp}
+        dc, di, dk = offset(d)
+        return {'cp': (c + cp - dc) % cp, 'tp': ((i + nx - di) % nx) * 2 + (k + dk) % 2}
 
     b = pltpu.get_barrier_semaphore()
 
@@ -413,8 +447,9 @@
         out_specs=spec(VMEM),
         scratch_shapes=[
             VMEM((nb // 2, HEAD, 2 * T), BF16), VMEM((tp, wo.shape[0], H), BF16),
-            VMEM((nx * cp, T, HEAD), BF16), VMEM((tp, T, 2 * HEAD), BF16),
-            DMA((10,)), DMA((10,)), DMA((nx * cp,)), DMA((nx * cp,)), DMA((2,)),
+            VMEM((2 * cp, 2, T, HEAD), BF16), VMEM((tp, T, 2 * HEAD), BF16),
+            VMEM((2 * T, 2 * T), F32), VMEM((2 * T, 2 * T), F32), VMEM((HEAD, 2 * T), F32),
+            DMA((10,)), DMA((10,)), DMA((2 * cp, 2)), DMA((2 * cp, 2)), DMA((2,)),
         ],
         compiler_params=params(1),
         name='attn',
@@ -427,7 +462,11 @@
     T, kk = idx.shape
     c = lax.axis_index('cp')
     t = lax.axis_index('tp')
-    rel = ((idx // tp - c + cp) % cp) * tp + (idx % tp - t + tp) % tp
+    nx = tp // 2
+    dc = (idx // tp - c + cp) % cp
+    di = (idx % tp // 2 - t // 2 + nx) % nx
+    dk = (idx % 2 + t % 2) % 2
+    rel = (((di - dc + nx) % nx) * cp + dc) * 2 + dk
     ea = rel.reshape(-1)
     onehot = (ea[:, None] == jnp.arange(ne)[None, :]).astype(jnp.int32)
     rank = jnp.cumsum(onehot, axis=0)

time: 306 us -> 262 us (0.86)
  Pallas kernels: 292 us -> 250 us
    pallas_call x1, Pallas kernels: 92.3 us -> 60.4 us  [attention(): pl.pallas_call(functools.partial(attn_kernel, cp, nx), out_shape=jax.Shap...]
    pallas_call x1, Pallas kernels: 144 us -> 134 us  [experts(): pl.pallas_call(functools.partial(moe_kernel, cp, tp, cap), out_shape=jax....]
where the time goes in v2:
time: 262 us; the launch traced here: 258 us
  Pallas kernels  250 us (95%)
  local copies, waits for them, and re-layouts  4.28 us (2%)
  other arithmetic  4.1 us (2%)
    pallas_call x1, Pallas kernels, experts(): pl.pallas_call(functools.partial(moe_kernel, cp, tp, cap), out_shape=jax....  134 us
    pallas_call x1, Pallas kernels, attention(): pl.pallas_call(functools.partial(attn_kernel, cp, nx), out_shape=jax.Shap...  60.4 us
    pallas_call x1, Pallas kernels, attention(): pl.pallas_call(functools.partial(qkv_kernel, cp, nx), out_shape=jax.Shape...  55.8 us

profile of v2, /device:TPU:111, one launch (start us, length us, event | category | flops | bytes accessed | tf_op | source)
XLA Modules:
  0.0 258.3 jit_solution(9919774210547339669)
XLA Ops:
  0.0 55.8 %qkv.1.kvq = bf16[32,3,256,128]{3,2,1,0:T(8,128)(2,1)} custom-call(bf16[256,2048]{1,0:T(8,128)(2,1)} %x_ref.3, bf16[2048,256]{1,0:T(8,128)(2,1)} %wq_ref.1, bf16[2048,256]{1,0:T(8,128)(2,1)} %wk_ref.1, bf16[2048,256]{1,0:T(8,128)(2,1)} %wv_ref.1), custom_call_target="tpu_custom_call" | custom-call | tf_op jit(solution)/shard_map/qkv/pallas_call | solution.py:430
  55.8 0.0 copy-start
  55.8 0.0 copy-start.1
  55.8 60.4 %attn.1.h_ref = bf16[256,2048]{1,0:T(8,128)(2,1)} custom-call(bf16[32,3,256,128]{3,2,1,0:T(8,128)(2,1)} %qkv.1.kvq, bf16[256,2048]{1,0:T(8,128)(2,1)} %wo_ref.1, bf16[256,2048]{1,0:T(8,128)(2,1)} %x_ref.3), custom_call_target="tpu_custom_call" | custom-call | tf_op jit(solution)/shard_map/attn/pallas_call | solution.py:443
  116.2 0.0 copy-done
  116.2 0.2 copy.26
  116.4 0.1 copy.23
  116.6 0.5 fusion.17
  117.0 0.1 eq.90
  117.2 0.1 eq.94
  117.3 1.2 reduce-window.6
  118.5 0.2 slice_reduce_fusion.2
  118.8 0.1 fusion.24
  118.9 0.1 sub.44
  119.1 0.2 slice_reduce_fusion.1
  119.3 1.0 fusion.1.p_ref
  120.3 1.3 fusion.2
  121.6 0.0 copy-done.1
  121.6 0.8 copy.31.gates_ref
  122.4 133.6 %moe.1 = bf16[256,2048]{1,0:T(8,128)(2,1)} custom-call(bf16[256,2048]{1,0:T(8,128)(2,1)} %attn.1.h_ref, bf16[1024,256]{1,0:T(8,128)(2,1)} %fusion.1.p_ref, bf16[256,1024]{1,0:T(8,128)(2,1)} %get-tuple-element.7.g0_ref, bf16[256,1024]{1,0:T(8,128)(2,1)} %get-tuple-element.8.g1_ref, f32[256,2]{1,0:T(8,128)} %copy.31.gates_ref, bf16[1,2048,1024]{2,1,0:T(8,128)(2,1)} %wg_hbm.1, ...), custom_call_target="tpu_custom_call" | custom-call | tf_op jit(solution)/shard_map/moe/pallas_call | solution.py:488
  256.0 2.3 copy.41
  (6 shorter events, 0.1 us)
Async XLA Ops:
  55.8 60.4 %copy-start = (s32[256,2]{0,1:T(2,128)S(1)}, s32[256,2]{0,1:T(2,128)}, u32[]{:S(2)}) copy-start(s32[256,2]{0,1:T(2,128)} %param.11) | copy-start | bytes 6148
  55.8 65.8 %copy-start.1 = (f32[256,2]{0,1:T(2,128)S(1)}, f32[256,2]{0,1:T(2,128)}, u32[]{:S(2)}) copy-start(f32[256,2]{0,1:T(2,128)} %param.12) | copy-start | bytes 6148

commit v3 on v2

--- a/solution.py
+++ b/solution.py
@@ -37,19 +37,66 @@
     return seg * 4 + (chip % 2) * 2 + core
 
 
-def qkv_kernel(cp, nx, x_ref, wq_ref, wk_ref, wv_ref, kvq, wsib, xb, stage, wss, wrs, xss, xrs, ass, ars, rss, rrs, ls):
+def slots(cp, nx, cap, c, i, k, idx_ref, pcol_ref, prow_ref):
+    T = idx_ref.shape[0]
+    tp = 2 * nx
+    ne = cp * tp
+    sh = tp.bit_length() - 1
+    e = idx_ref[...]
+    dc = ((e >> sh) - c) & (cp - 1)
+    di = (((e & (tp - 1)) >> 1) - i) & (nx - 1)
+    dk = (e - k) & 1
+    rel = ((((di - dc) & (nx - 1)) * cp + dc) * 2 + dk)
+    lanes = lax.broadcasted_iota(jnp.int32, (T, ne), 1)
+    o0 = (rel[:, 0:1] == lanes).astype(F32)
+    o1 = (rel[:, 1:2] == lanes).astype(F32)
+    low = lax.broadcasted_iota(jnp.int32, (T, T), 0) > lax.broadcasted_iota(jnp.int32, (T, T), 1)
+    prev = jnp.dot(low.astype(F32).astype(BF16), (o0 + o1).astype(BF16), preferred_element_type=F32)
+    p0 = rel[:, 0:1] * cap + jnp.sum(prev * o0, axis=1, keepdims=True).astype(jnp.int32)
+    p1 = rel[:, 1:2] * cap + jnp.sum(prev * o1, axis=1, keepdims=True).astype(jnp.int32)
+    pcol_ref[:, 0:1] = p0
+    pcol_ref[:, 1:2] = p1
+    wide = (T, HEAD)
+    prow_ref[0:1, :] = jnp.broadcast_to(p0.astype(F32), wide).T[0:1, :].astype(jnp.int32)
+    prow_ref[1:2, :] = jnp.broadcast_to(p1.astype(F32), wide).T[0:1, :].astype(jnp.int32)
+
+
+def attn_kernel(cp, nx, cap, x_ref, wq_ref, wk_ref, wv_ref, wo_ref, idx_ref, h_ref, pcol_ref, prow_ref,
+                kvq, wsib, xb, stage, vt, wof, ostage, obuf, sa, sb, acc,
+                wss, wrs, xss, xrs, ass, ars, rss, rrs, qls, wos, wor, oss, ors, ls):
     c = lax.axis_index('cp')
     t = lax.axis_index('tp')
     i, k = t // 2, t % 2
-    T = x_ref.shape[0]
+    T, H = x_ref.shape
     half = T // 2
     sib = {'cp': c, 'tp': i * 2 + 1 - k}
     right = {'cp': c, 'tp': ((i + 1) % nx) * 2 + k}
     left = {'cp': c, 'tp': ((i + nx - 1) % nx) * 2 + k}
     peer = [{'cp': (c + d) % cp, 'tp': t} for d in range(cp)]
-    barrier_with([sib, right, left] + peer[1:])
+    same = [{'cp': (c + dc) % cp, 'tp': ((i + di) % nx) * 2 + k} for di in range(nx) for dc in range(cp)]
+    barrier_with([sib] + same[1:])
     lo, hi = pl.ds(0, half), pl.ds(half, half)
     full = pl.ds(0, T)
+
+    R = wo_ref.shape[0]
+    hr = R // 2
+    rlo, rhi, rfull = pl.ds(0, hr), pl.ds(hr, hr), pl.ds(0, R)
+    ri, li, oi = (i + 1) % nx, (i + nx - 1) % nx, (i + 2) % nx
+    def wcopy(n, src, chip, core, rows, to):
+        return remote(src, wof.at[chip * 2 + core, rows], wos.at[n], wor.at[n], to)
+
+    w0 = wcopy(0, wo_ref.at[rlo], i, k, rlo, right)
+    w1 = wcopy(1, wo_ref.at[rhi], i, k, rhi, left)
+    w2 = wcopy(2, wo_ref.at[rhi], i, k, rhi, right)
+    w3 = wcopy(3, wo_ref.at[rlo], i, k, rlo, left)
+    w6 = wcopy(6, wo_ref, i, k, rfull, sib)
+    wl = pltpu.make_async_copy(wo_ref, wof.at[t], ls.at[0])
+    w4 = wcopy(4, wof.at[li * 2 + k, rlo], li, k, rlo, right)
+    w5 = wcopy(5, wof.at[ri * 2 + k, rhi], ri, k, rhi, left)
+    w7 = wcopy(7, wof.at[li * 2 + k], li, k, rfull, sib)
+    w8 = wcopy(8, wof.at[ri * 2 + k], ri, k, rfull, sib)
+    w9 = wcopy(9, wof.at[oi * 2 + k], oi, k, rfull, sib)
+
 
     def xcopy(n, src, slot, rows, dev):
         return remote(src.at[rows], xb.at[slot, rows], xss.at[n], xrs.at[n], dev)
@@ -92,7 +139,7 @@
             cps = remote(stage.at[u, (c + d) % cp, :, rows], kvq.at[b, :, rows], ass.at[u, d], ars.at[u, d], peer[d])
             cps.start()
             pend.append(cps)
-        lc = pltpu.make_async_copy(stage.at[u, c, :, rows], kvq.at[b, :, rows], ls.at[u])
+        lc = pltpu.make_async_copy(stage.at[u, c, :, rows], kvq.at[b, :, rows], qls.at[u])
         lc.start()
         locs.append(lc)
         relay(u, 0, stage.at[u, c, pl.ds(1, 2), rows])
@@ -115,6 +162,7 @@
     locs = []
     compute(0, x_ref, full)
     send(0)
+    slots(cp, nx, cap, c, i, k, idx_ref, pcol_ref, prow_ref)
     sends[0].wait_recv()
     f = xcopy(4, xb.at[0], 2, lo, right)
     f.start()
@@ -122,6 +170,9 @@
     sends[1].wait_recv()
     g.start()
     pend += [f, g]
+    for w in (w0, w1, w2, w3, w6):
+        w.start()
+    wl.start()
     compute(1, xb.at[0], lo)
     send(1)
     compute(2, xb.at[1], hi)
@@ -149,46 +200,12 @@
         remote(stage.at[u, 0, pl.ds(1, 2), rows], kvq.at[b, pl.ds(1, 2), rows], rss.at[u, d], rrs.at[u, d], sib).wait_recv()
     for lc in locs:
         lc.wait()
-    for s in pend:
-        s.wait_send()
-
-
-def attn_kernel(cp, nx, kvq, wo_ref, x_ref, h_ref, vt, wof, ostage, obuf, sa, sb, acc, wss, wrs, oss, ors, ls):
-    c = lax.axis_index('cp')
-    t = lax.axis_index('tp')
-    i, k = t // 2, t % 2
-    T, H = x_ref.shape
-    R = wo_ref.shape[0]
+
+    w0.wait_recv()
+    w4.start()
+    w1.wait_recv()
+    w5.start()
     nch = kvq.shape[0] // 2
-    sib = {'cp': c, 'tp': i * 2 + 1 - k}
-    ri, li, oi = (i + 1) % nx, (i + nx - 1) % nx, (i + 2) % nx
-    right = {'cp': c, 'tp': ri * 2 + k}
-    left = {'cp': c, 'tp': li * 2 + k}
-    offs = [(di, dc) for di in range(nx) for dc in range(cp)]
-
-    def dev(di, dc):
-        return {'cp': (c + dc) % cp, 'tp': ((i + di) % nx) * 2 + k}
-
-    barrier_with([sib] + [dev(di, dc) for di, dc in offs[1:]])
-    half = R // 2
-    lo, hi, full = pl.ds(0, half), pl.ds(half, half), pl.ds(0, R)
-    def wcopy(n, src, chip, core, rows, to):
-        return remote(src, wof.at[chip * 2 + core, rows], wss.at[n], wrs.at[n], to)
-
-    w0 = wcopy(0, wo_ref.at[lo], i, k, lo, right)
-    w1 = wcopy(1, wo_ref.at[hi], i, k, hi, left)
-    w2 = wcopy(2, wo_ref.at[hi], i, k, hi, right)
-    w3 = wcopy(3, wo_ref.at[lo], i, k, lo, left)
-    w6 = wcopy(6, wo_ref, i, k, full, sib)
-    for w in (w0, w1, w2, w3, w6):
-        w.start()
-    wl = pltpu.make_async_copy(wo_ref, wof.at[t], ls.at[0])
-    wl.start()
-    w4 = wcopy(4, wof.at[li * 2 + k, lo], li, k, lo, right)
-    w5 = wcopy(5, wof.at[ri * 2 + k, hi], ri, k, hi, left)
-    w7 = wcopy(7, wof.at[li * 2 + k], li, k, full, sib)
-    w8 = wcopy(8, wof.at[ri * 2 + k], ri, k, full, sib)
-    w9 = wcopy(9, wof.at[oi * 2 + k], oi, k, full, sib)
 
     @pl.loop(0, nch)
     def _(m):
@@ -259,17 +276,12 @@
             osend(n, 0).start()
             osend(n, 1).start()
 
-    run(1, 3)
-    w0.wait_recv()
-    w4.start()
-    w1.wait_recv()
-    w5.start()
-    run(3, 5)
+    run(1, 4)
     w2.wait_recv()
     w7.start()
     w3.wait_recv()
     w8.start()
-    run(5, npair)
+    run(4, npair)
     attend(0)
     osend(0, 1).start()
     lo_c = pltpu.make_async_copy(ostage.at[0, 0], obuf.at[i * 2 + c // 2, :, col], ls.at[1])
@@ -306,10 +318,12 @@
     def _(n):
         osend(n, 0).wait_send()
         osend(n, 1).wait_send()
-
-
-def moe_kernel(cp, tp, cap, h_ref, p_ref, g0_ref, g1_ref, gates_ref, wg_hbm, wu_hbm, wd_hbm, y_ref,
-               sendb, recvb, zb, back, wg, wu, wd, acc0, acc1, wsem, dss, drs, bss, brs):
+    for s in pend:
+        s.wait_send()
+
+
+def moe_kernel(cp, tp, cap, h_ref, pcol_ref, prow_ref, gates_ref, wg_hbm, wu_hbm, wd_hbm, y_ref,
+               sendb, recvb, zb, back, wg, wu, wd, acc, wsem, dss, drs, bss, brs):
     c = lax.axis_index('cp')
     t = lax.axis_index('tp')
     ne = cp * tp
@@ -342,8 +356,9 @@
         pl.semaphore_signal(b, inc=1, device_id=fwd(d), device_id_type=MESH)
 
     def pack(g):
-        rows = p_ref[pl.ds(g * grp * cap, grp * cap), :]
-        r = jnp.dot(rows, h_ref[...], preferred_element_type=F32).astype(BF16)
+        s = lax.broadcasted_iota(jnp.int32, (grp * cap, T), 0) + g * (grp * cap)
+        pick = jnp.where((s == prow_ref[0:1, :]) | (s == prow_ref[1:2, :]), 1.0, 0.0).astype(BF16)
+        r = jnp.dot(pick, h_ref[...], preferred_element_type=F32).astype(BF16)
         sendb[pl.ds(g * grp, grp)] = r.reshape(grp, cap, H)
 
     def disp(d):
@@ -377,9 +392,11 @@
 
     def combine(g):
         zz = back[pl.ds(g * grp, grp)].reshape(grp * cap, H)
-        cols = pl.ds(pl.multiple_of(g * grp * cap, grp * cap), grp * cap)
-        return (jnp.dot(g0_ref[:, cols], zz, preferred_element_type=F32),
-                jnp.dot(g1_ref[:, cols], zz, preferred_element_type=F32))
+        s = lax.broadcasted_iota(jnp.int32, (T, grp * cap), 1) + g * (grp * cap)
+        g0 = jnp.where(s == pcol_ref[:, 0:1], 1.0, 0.0).astype(BF16)
+        g1 = jnp.where(s == pcol_ref[:, 1:2], 1.0, 0.0).astype(BF16)
+        return (gates_ref[:, 0:1] * jnp.dot(g0, zz, preferred_element_type=F32)
+                + gates_ref[:, 1:2] * jnp.dot(g1, zz, preferred_element_type=F32))
 
     for d in range(1, grp):
         disp(d).wait_recv()
@@ -398,19 +415,15 @@
 
     for d in range(1, grp):
         ret(d).wait_recv()
-    a, bb = combine(0)
-    acc0[...] = a
-    acc1[...] = bb
+    acc[...] = h_ref[...].astype(F32) + combine(0)
 
     @pl.loop(1, ng)
     def _(g):
         for j in range(grp):
             ret(g * grp + j).wait_recv()
-        a, bb = combine(g)
-        acc0[...] += a
-        acc1[...] += bb
-
-    y_ref[...] = (h_ref[...].astype(F32) + (gates_ref[:, 0:1] * acc0[...] + gates_ref[:, 1:2] * acc1[...])).astype(BF16)
+        acc[...] += combine(g)
+
+    y_ref[...] = acc[...].astype(BF16)
 
     @pl.loop(1, ne)
     def _(d):
@@ -422,81 +435,48 @@
     return pltpu.CompilerParams(collective_id=cid, has_side_effects=True, vmem_limit_bytes=60 * 1024 * 1024)
 
 
-def attention(x, wq, wk, wv, wo, cp, tp):
+def attention(x, idx, wq, wk, wv, wo, cp, tp, cap):
     T, H = x.shape
     nx = tp // 2
     nb = cp * tp
     W = wq.shape[1]
-    kvq = pl.pallas_call(
-        functools.partial(qkv_kernel, cp, nx),
-        out_shape=jax.ShapeDtypeStruct((nb, 3, T, HEAD), BF16),
-        in_specs=[spec(VMEM)] * 4,
-        out_specs=spec(VMEM),
+    return pl.pallas_call(
+        functools.partial(attn_kernel, cp, nx, cap),
+        out_shape=[
+            jax.ShapeDtypeStruct((T, H), BF16), jax.ShapeDtypeStruct(idx.shape, jnp.int32), jax.ShapeDtypeStruct((2, T), jnp.int32),
+        ],
+        in_specs=[spec(VMEM)] * 6,
+        out_specs=[spec(VMEM)] * 3,
         scratch_shapes=[
-            VMEM((3, H, W), BF16), VMEM((3, T, H), BF16), VMEM((7, 4, 3, T, HEAD), BF16),
-            DMA((3,)), DMA((3,)), DMA((6,)), DMA((6,)),
-            DMA((7, cp)), DMA((7, cp)), DMA((7, cp)), DMA((7, cp)), DMA((7,)),
-        ],
-        compiler_params=params(0),
-        name='qkv',
-    )(x, wq, wk, wv)
-    h = pl.pallas_call(
-        functools.partial(attn_kernel, cp, nx),
-        out_shape=jax.ShapeDtypeStruct((T, H), BF16),
-        in_specs=[spec(VMEM)] * 3,
-        out_specs=spec(VMEM),
-        scratch_shapes=[
+            VMEM((nb, 3, T, HEAD), BF16), VMEM((3, H, W), BF16), VMEM((3, T, H), BF16), VMEM((7, 4, 3, T, HEAD), BF16),
             VMEM((nb // 2, HEAD, 2 * T), BF16), VMEM((tp, wo.shape[0], H), BF16),
             VMEM((2 * cp, 2, T, HEAD), BF16), VMEM((tp, T, 2 * HEAD), BF16),
             VMEM((2 * T, 2 * T), F32), VMEM((2 * T, 2 * T), F32), VMEM((HEAD, 2 * T), F32),
+            DMA((3,)), DMA((3,)), DMA((6,)), DMA((6,)),
+            DMA((7, cp)), DMA((7, cp)), DMA((7, cp)), DMA((7, cp)), DMA((7,)),
             DMA((10,)), DMA((10,)), DMA((2 * cp, 2)), DMA((2 * cp, 2)), DMA((2,)),
         ],
-        compiler_params=params(1),
+        compiler_params=params(0),
         name='attn',
-    )(kvq, wo, x)
-    return h
-
-
-def routing(idx, cp, tp, cap):
-    ne = cp * tp
-    T, kk = idx.shape
-    c = lax.axis_index('cp')
-    t = lax.axis_index('tp')
-    nx = tp // 2
-    dc = (idx // tp - c + cp) % cp
-    di = (idx % tp // 2 - t // 2 + nx) % nx
-    dk = (idx % 2 + t % 2) % 2
-    rel = (((di - dc + nx) % nx) * cp + dc) * 2 + dk
-    ea = rel.reshape(-1)
-    onehot = (ea[:, None] == jnp.arange(ne)[None, :]).astype(jnp.int32)
-    rank = jnp.cumsum(onehot, axis=0)
-    slot = jnp.sum(onehot * rank, axis=1) - 1
-    pos = (ea * cap + slot).reshape(T, kk)
-    cols = jnp.arange(ne * cap, dtype=jnp.int32)
-    g0 = pos[:, 0:1] == cols[None, :]
-    g1 = pos[:, 1:2] == cols[None, :]
-    p = (pos[:, 0][None, :] == cols[:, None]) | (pos[:, 1][None, :] == cols[:, None])
-    return p.astype(BF16), g0.astype(BF16), g1.astype(BF16)
-
-
-def experts(h, idx, gates, w1g, w1u, w2, cp, tp):
+    )(x, wq, wk, wv, wo, idx)
+
+
+def experts(h, pcol, prow, gates, w1g, w1u, w2, cp, tp, cap):
     T, H = h.shape
     F = w1g.shape[2]
     ne = cp * tp
-    cap = 4 * T // ne
-    p, g0, g1 = routing(idx, cp, tp, cap)
     return pl.pallas_call(
         functools.partial(moe_kernel, cp, tp, cap),
         out_shape=jax.ShapeDtypeStruct((T, H), BF16),
-        in_specs=[spec(VMEM)] * 5 + [spec(pl.ANY)] * 3,
+        in_specs=[spec(VMEM)] * 4 + [spec(pl.ANY)] * 3,
         out_specs=spec(VMEM),
         scratch_shapes=[VMEM((ne, cap, H), BF16)] * 4 + [
-            VMEM((H, F), BF16), VMEM((H, F), BF16), VMEM((F, H), BF16), VMEM((T, H), F32), VMEM((T, H), F32),
+            VMEM((H, F), BF16), VMEM((H, F), BF16), VMEM((F, H), BF16), VMEM((T, H), F32),
             DMA((3,)), DMA((ne,)), DMA((ne,)), DMA((ne,)), DMA((ne,)),
         ],
-        compiler_params=params(2),
+        compiler_params=params(1),
         name='moe',
-    )(h, p, g0, g1, gates, w1g, w1u, w2)
+    )(h, pcol, prow, gates, w1g, w1u, w2)
 
 
 def solution(mesh):
@@ -506,7 +486,8 @@
     exp_spec = P(('cp', 'tp'), None, None)
 
     def local(x, idx, gates, wq, wk, wv, wo, w1g, w1u, w2):
-        h = attention(x, wq, wk, wv, wo, cp, tp)
-        return experts(h, idx, gates, w1g, w1u, w2, cp, tp)
+        cap = 4 * x.shape[0] // (cp * tp)
+        h, pcol, prow = attention(x, idx, wq, wk, wv, wo, cp, tp, cap)
+        return experts(h, pcol, prow, gates, w1g, w1u, w2, cp, tp, cap)
 
     return jax.shard_map(local, mesh=mesh, in_specs=(rows_spec, rows_spec, rows_spec, P(None, 'tp'), P(None, 'tp'), P(None, 'tp'), P('tp', None), exp_spec, exp_spec, exp_spec), out_specs=rows_spec, check_vma=False)

time: 262 us -> 233 us (0.89); the launches traced: 258 us -> 233 us
  Pallas kernels: 250 us -> 228 us
  other arithmetic: 4.1 us -> 0 us
    pallas_call x2 -> x1, Pallas kernels: 116 us -> 95.5 us  [attention(): pl.pallas_call(functools.partial(attn_kernel, cp, nx, cap), out_shape=[ja...]
    unnamed x7 -> x3, local copies, waits for them, and re-layouts: 3.25 us -> 5.25 us
where the time goes in v3:
time: 233 us
  Pallas kernels  228 us (98%)
  local copies, waits for them, and re-layouts  5.25 us (2%)
    pallas_call x1, Pallas kernels, experts(): pl.pallas_call(functools.partial(moe_kernel, cp, tp, cap), out_shape=jax....  132 us
    pallas_call x1, Pallas kernels, attention(): pl.pallas_call(functools.partial(attn_kernel, cp, nx, cap), out_shape=[ja...  95.5 us
    unnamed x3, local copies, waits for them, and re-layouts  5.25 us

profile of v3, /device:TPU:111, one launch (start us, length us, event | category | flops | bytes accessed | tf_op | source)
XLA Modules:
  0.0 233.0 jit_solution(8802228623864158726)
XLA Ops:
  0.0 1.5 copy.11.idx_ref
  1.5 1.5 copy.12.gates_ref
  2.9 95.5 %attn.1 = (bf16[256,2048]{1,0:T(8,128)(2,1)}, s32[256,2]{1,0:T(8,128)}, s32[2,256]{1,0:T(2,128)}) custom-call(bf16[256,2048]{1,0:T(8,128)(2,1)} %x_ref.1, bf16[2048,256]{1,0:T(8,128)(2,1)} %wq_ref.1, bf16[2048,256]{1,0:T(8,128)(2,1)} %wk_ref.1, bf16[2048,256]{1,0:T(8,128)(2,1)} %wv_ref.1, bf16[256,2048]{1,0:T(8,128)(2,1)} %wo_ref.1, s32[256,2]{1,0:T(8,128)} %copy.11.idx_ref), custom_call_target="tpu_custom_call" | custom-call | tf_op jit(solution)/shard_map/attn/pallas_call | solution.py:443
  98.4 132.3 %moe.1 = bf16[256,2048]{1,0:T(8,128)(2,1)} custom-call(bf16[256,2048]{1,0:T(8,128)(2,1)} %get-tuple-element.8.h_ref, s32[256,2]{1,0:T(8,128)} %get-tuple-element.9.pcol_ref, s32[2,256]{1,0:T(2,128)} %get-tuple-element.10.prow_ref, f32[256,2]{1,0:T(8,128)} %copy.12.gates_ref, bf16[1,2048,1024]{2,1,0:T(8,128)(2,1)} %wg_hbm.1, bf16[1,2048,1024]{2,1,0:T(8,128)(2,1)} %wu_hbm.1, ...), custom_call_target="tpu_custom_call" | custom-call | tf_op jit(solution)/shard_map/moe/pallas_call | solution.py:468
  230.7 2.3 copy.14

commit v4 on v3

--- a/solution.py
+++ b/solution.py
@@ -37,8 +37,8 @@
     return seg * 4 + (chip % 2) * 2 + core
 
 
-def slots(cp, nx, cap, c, i, k, idx_ref, pcol_ref, prow_ref):
-    T = idx_ref.shape[0]
+def slots(cp, nx, cap, c, i, k, idx_ref, prow_ref):
+    T = idx_ref.shape[1]
     tp = 2 * nx
     ne = cp * tp
     sh = tp.bit_length() - 1
@@ -47,21 +47,18 @@
     di = (((e & (tp - 1)) >> 1) - i) & (nx - 1)
     dk = (e - k) & 1
     rel = ((((di - dc) & (nx - 1)) * cp + dc) * 2 + dk)
-    lanes = lax.broadcasted_iota(jnp.int32, (T, ne), 1)
-    o0 = (rel[:, 0:1] == lanes).astype(F32)
-    o1 = (rel[:, 1:2] == lanes).astype(F32)
-    low = lax.broadcasted_iota(jnp.int32, (T, T), 0) > lax.broadcasted_iota(jnp.int32, (T, T), 1)
-    prev = jnp.dot(low.astype(F32).astype(BF16), (o0 + o1).astype(BF16), preferred_element_type=F32)
-    p0 = rel[:, 0:1] * cap + jnp.sum(prev * o0, axis=1, keepdims=True).astype(jnp.int32)
-    p1 = rel[:, 1:2] * cap + jnp.sum(prev * o1, axis=1, keepdims=True).astype(jnp.int32)
-    pcol_ref[:, 0:1] = p0
-    pcol_ref[:, 1:2] = p1
-    wide = (T, HEAD)
-    prow_ref[0:1, :] = jnp.broadcast_to(p0.astype(F32), wide).T[0:1, :].astype(jnp.int32)
-    prow_ref[1:2, :] = jnp.broadcast_to(p1.astype(F32), wide).T[0:1, :].astype(jnp.int32)
-
-
-def attn_kernel(cp, nx, cap, x_ref, wq_ref, wk_ref, wv_ref, wo_ref, idx_ref, h_ref, pcol_ref, prow_ref,
+    experts_i = lax.broadcasted_iota(jnp.int32, (ne, T), 0)
+    o0 = (rel[0:1, :] == experts_i).astype(F32)
+    o1 = (rel[1:2, :] == experts_i).astype(F32)
+    low = lax.broadcasted_iota(jnp.int32, (T, T), 0) < lax.broadcasted_iota(jnp.int32, (T, T), 1)
+    prev = jnp.dot((o0 + o1).astype(BF16), low.astype(F32).astype(BF16), preferred_element_type=F32)
+    p0 = rel[0:1, :] * cap + jnp.sum(prev * o0, axis=0, keepdims=True).astype(jnp.int32)
+    p1 = rel[1:2, :] * cap + jnp.sum(prev * o1, axis=0, keepdims=True).astype(jnp.int32)
+    prow_ref[0:1, :] = p0
+    prow_ref[1:2, :] = p1
+
+
+def attn_kernel(cp, nx, cap, x_ref, wq_ref, wk_ref, wv_ref, wo_ref, idx_ref, h_ref, prow_ref,
                 kvq, wsib, xb, stage, vt, wof, ostage, obuf, sa, sb, acc,
                 wss, wrs, xss, xrs, ass, ars, rss, rrs, qls, wos, wor, oss, ors, ls):
     c = lax.axis_index('cp')
@@ -162,7 +159,7 @@
     locs = []
     compute(0, x_ref, full)
     send(0)
-    slots(cp, nx, cap, c, i, k, idx_ref, pcol_ref, prow_ref)
+    slots(cp, nx, cap, c, i, k, idx_ref, prow_ref)
     sends[0].wait_recv()
     f = xcopy(4, xb.at[0], 2, lo, right)
     f.start()
@@ -218,17 +215,18 @@
     qpos = col_i % T + k * T + 2 * T * jnp.where(col_i < T, par, 1 - par)
     row_i = lax.broadcasted_iota(jnp.int32, (2 * T, 2 * T), 0)
 
-    def scores(q, m, buf):
+    def scores(q, m, part, buf):
         kb = kvq[pl.ds(2 * m, 2), 1].reshape(2 * T, HEAD)
-        buf[...] = lax.dot_general(kb, q, (((1,), (1,)), ((), ())), preferred_element_type=F32)
-
-    def absorb(buf, m, part, ml):
-        mo, l = ml
-        s = buf[...]
+        s = lax.dot_general(kb, q, (((1,), (1,)), ((), ())), preferred_element_type=F32)
         if part is not None:
             s = jnp.where(row_i + 2 * T * part <= qpos, s, -jnp.inf)
-        mn = jnp.maximum(mo, jnp.max(s, axis=0, keepdims=True))
-        w = jnp.exp2((s - mn) * scale)
+        buf[...] = s
+        return jnp.max(s, axis=0, keepdims=True)
+
+    def absorb(buf, m, top, ml):
+        mo, l = ml
+        mn = jnp.maximum(mo, top)
+        w = jnp.exp2((buf[...] - mn) * scale)
         a = jnp.exp2((mo - mn) * scale)
         l = l * a + jnp.sum(w, axis=0, keepdims=True)
         acc[...] = acc[...] * a + jnp.dot(vt[m], w.astype(BF16), preferred_element_type=F32)
@@ -242,19 +240,24 @@
         q = jnp.concatenate([kvq[pb0, 0], kvq[pb1, 0]], axis=0)
         p = pb0 // 4
         acc[...] = jnp.zeros_like(acc)
-        scores(q, 0, sa)
-
-        def body(j, ml):
-            scores(q, 2 * j + 1, sb)
-            ml = absorb(sa, 2 * j, None, ml)
-            scores(q, 2 * j + 2, sa)
-            return absorb(sb, 2 * j + 1, None, ml)
+        last = p * 2
+
+        def body(j, carry):
+            ml, ta = carry
+            tb = scores(q, 2 * j + 1, None, sb)
+            ml = absorb(sa, 2 * j, ta, ml)
+            ta = scores(q, 2 * j + 2, None, sa)
+            return absorb(sb, 2 * j + 1, tb, ml), ta
 
         ml = (jnp.full((1, 2 * T), -jnp.inf, F32), jnp.zeros((1, 2 * T), F32))
-        ml = lax.fori_loop(0, p, body, ml)
-        scores(q, 2 * p + 1, sb)
-        ml = absorb(sa, 2 * p, 0, ml)
-        _, l = absorb(sb, 2 * p + 1, 1, ml)
+        ta = scores(q, 0, None, sa)
+        ml, ta = lax.fori_loop(0, p, body, (ml, ta))
+        s = jnp.where(row_i <= qpos, sa[...], -jnp.inf)
+        sa[...] = s
+        ta = jnp.max(s, axis=0, keepdims=True)
+        tb = scores(q, last + 1, 1, sb)
+        ml = absorb(sa, last, ta, ml)
+        _, l = absorb(sb, last + 1, tb, ml)
         o = (acc[...] / l).T.astype(BF16)
         ostage[n, 0] = o[:T]
         ostage[n, 1] = o[T:]
@@ -322,8 +325,8 @@
         s.wait_send()
 
 
-def moe_kernel(cp, tp, cap, h_ref, pcol_ref, prow_ref, gates_ref, wg_hbm, wu_hbm, wd_hbm, y_ref,
-               sendb, recvb, zb, back, wg, wu, wd, acc, wsem, dss, drs, bss, brs):
+def moe_kernel(cp, tp, cap, h_ref, prow_ref, gates_ref, wg_hbm, wu_hbm, wd_hbm, y_ref,
+               sendb, recvb, zb, back, wg, wu, wd, acc, colb, wsem, dss, drs, bss, brs):
     c = lax.axis_index('cp')
     t = lax.axis_index('tp')
     ne = cp * tp
@@ -379,6 +382,8 @@
         for j in range(grp):
             disp(g * grp + j).start()
 
+    rows4 = jnp.concatenate([prow_ref[...].astype(F32), gates_ref[...], jnp.zeros((HEAD - 4, T), F32)], axis=0)
+    colb[...] = rows4.T
     for w in wc:
         w.wait()
 
@@ -393,10 +398,10 @@
     def combine(g):
         zz = back[pl.ds(g * grp, grp)].reshape(grp * cap, H)
         s = lax.broadcasted_iota(jnp.int32, (T, grp * cap), 1) + g * (grp * cap)
-        g0 = jnp.where(s == pcol_ref[:, 0:1], 1.0, 0.0).astype(BF16)
-        g1 = jnp.where(s == pcol_ref[:, 1:2], 1.0, 0.0).astype(BF16)
-        return (gates_ref[:, 0:1] * jnp.dot(g0, zz, preferred_element_type=F32)
-                + gates_ref[:, 1:2] * jnp.dot(g1, zz, preferred_element_type=F32))
+        g0 = jnp.where(s == colb[:, 0:1].astype(jnp.int32), 1.0, 0.0).astype(BF16)
+        g1 = jnp.where(s == colb[:, 1:2].astype(jnp.int32), 1.0, 0.0).astype(BF16)
+        return (colb[:, 2:3] * jnp.dot(g0, zz, preferred_element_type=F32)
+                + colb[:, 3:4] * jnp.dot(g1, zz, preferred_element_type=F32))
 
     for d in range(1, grp):
         disp(d).wait_recv()
@@ -443,10 +448,10 @@
     return pl.pallas_call(
         functools.partial(attn_kernel, cp, nx, cap),
         out_shape=[
-            jax.ShapeDtypeStruct((T, H), BF16), jax.ShapeDtypeStruct(idx.shape, jnp.int32), jax.ShapeDtypeStruct((2, T), jnp.int32),
+            jax.ShapeDtypeStruct((T, H), BF16), jax.ShapeDtypeStruct((2, T), jnp.int32),
         ],
         in_specs=[spec(VMEM)] * 6,
-        out_specs=[spec(VMEM)] * 3,
+        out_specs=[spec(VMEM)] * 2,
         scratch_shapes=[
             VMEM((nb, 3, T, HEAD), BF16), VMEM((3, H, W), BF16), VMEM((3, T, H), BF16), VMEM((7, 4, 3, T, HEAD), BF16),
             VMEM((nb // 2, HEAD, 2 * T), BF16), VMEM((tp, wo.shape[0], H), BF16),
@@ -458,25 +463,25 @@
         ],
         compiler_params=params(0),
         name='attn',
-    )(x, wq, wk, wv, wo, idx)
-
-
-def experts(h, pcol, prow, gates, w1g, w1u, w2, cp, tp, cap):
+    )(x, wq, wk, wv, wo, idx.T)
+
+
+def experts(h, prow, gates, w1g, w1u, w2, cp, tp, cap):
     T, H = h.shape
     F = w1g.shape[2]
     ne = cp * tp
     return pl.pallas_call(
         functools.partial(moe_kernel, cp, tp, cap),
         out_shape=jax.ShapeDtypeStruct((T, H), BF16),
-        in_specs=[spec(VMEM)] * 4 + [spec(pl.ANY)] * 3,
+        in_specs=[spec(VMEM)] * 3 + [spec(pl.ANY)] * 3,
         out_specs=spec(VMEM),
         scratch_shapes=[VMEM((ne, cap, H), BF16)] * 4 + [
-            VMEM((H, F), BF16), VMEM((H, F), BF16), VMEM((F, H), BF16), VMEM((T, H), F32),
+            VMEM((H, F), BF16), VMEM((H, F), BF16), VMEM((F, H), BF16), VMEM((T, H), F32), VMEM((T, HEAD), F32),
             DMA((3,)), DMA((ne,)), DMA((ne,)), DMA((ne,)), DMA((ne,)),
         ],
         compiler_params=params(1),
         name='moe',
-    )(h, pcol, prow, gates, w1g, w1u, w2)
+    )(h, prow, gates.T, w1g, w1u, w2)
 
 
 def solution(mesh):
@@ -487,7 +492,7 @@
 
     def local(x, idx, gates, wq, wk, wv, wo, w1g, w1u, w2):
         cap = 4 * x.shape[0] // (cp * tp)
-        h, pcol, prow = attention(x, idx, wq, wk, wv, wo, cp, tp, cap)
-        return experts(h, pcol, prow, gates, w1g, w1u, w2, cp, tp, cap)
+        h, prow = attention(x, idx, wq, wk, wv, wo, cp, tp, cap)
+        return experts(h, prow, gates, w1g, w1u, w2, cp, tp, cap)
 
     return jax.shard_map(local, mesh=mesh, in_specs=(rows_spec, rows_spec, rows_spec, P(None, 'tp'), P(None, 'tp'), P(None, 'tp'), P('tp', None), exp_spec, exp_spec, exp_spec), out_specs=rows_spec, check_vma=False)

time: 233 us -> 238 us (1.021)
  Pallas kernels: 228 us -> 235 us
  local copies, waits for them, and re-layouts: 5.25 us -> 2.3 us
    pallas_call x1, Pallas kernels: 132 us -> 139 us  [experts(): pl.pallas_call(functools.partial(moe_kernel, cp, tp, cap), out_shape=jax....]
    unnamed x3 -> x1, local copies, waits for them, and re-layouts: 5.25 us -> 2.3 us
where the time goes in v4:
time: 238 us; the launch traced here: 237 us
  Pallas kernels  235 us (99%)
    pallas_call x1, Pallas kernels, experts(): pl.pallas_call(functools.partial(moe_kernel, cp, tp, cap), out_shape=jax....  139 us
    pallas_call x1, Pallas kernels, attention(): pl.pallas_call(functools.partial(attn_kernel, cp, nx, cap), out_shape=[ja...  95.6 us

profile of v4, /device:TPU:111, one launch (start us, length us, event | category | flops | bytes accessed | tf_op | source)
XLA Modules:
  0.0 237.4 jit_solution(11696229511765503461)
XLA Ops:
  0.0 95.6 %attn.1 = (bf16[256,2048]{1,0:T(8,128)(2,1)}, s32[2,256]{1,0:T(2,128)}) custom-call(bf16[256,2048]{1,0:T(8,128)(2,1)} %x_ref.1, bf16[2048,256]{1,0:T(8,128)(2,1)} %wq_ref.1, bf16[2048,256]{1,0:T(8,128)(2,1)} %wk_ref.1, bf16[2048,256]{1,0:T(8,128)(2,1)} %wv_ref.1, bf16[256,2048]{1,0:T(8,128)(2,1)} %wo_ref.1, s32[2,256]{1,0:T(2,128)} %bitcast.2), custom_call_target="tpu_custom_call" | custom-call | tf_op jit(solution)/shard_map/attn/pallas_call | solution.py:448
  95.6 139.5 %moe.1 = bf16[256,2048]{1,0:T(8,128)(2,1)} custom-call(bf16[256,2048]{1,0:T(8,128)(2,1)} %get-tuple-element.7.h_ref, s32[2,256]{1,0:T(2,128)} %get-tuple-element.8.prow_ref, f32[2,256]{1,0:T(2,128)} %bitcast.3, bf16[1,2048,1024]{2,1,0:T(8,128)(2,1)} %wg_hbm.1, bf16[1,2048,1024]{2,1,0:T(8,128)(2,1)} %wu_hbm.1, bf16[1,1024,2048]{2,1,0:T(8,128)(2,1)} %wd_hbm.1), custom_call_target="tpu_custom_call" | custom-call | tf_op jit(solution)/shard_map/moe/pallas_call | solution.py:473
  235.1 2.3 copy.12

commit v5 on v4

--- a/solution.py
+++ b/solution.py
@@ -59,20 +59,18 @@
 
 
 def attn_kernel(cp, nx, cap, x_ref, wq_ref, wk_ref, wv_ref, wo_ref, idx_ref, h_ref, prow_ref,
-                kvq, wsib, xb, stage, vt, wof, ostage, obuf, sa, sb, acc,
-                wss, wrs, xss, xrs, ass, ars, rss, rrs, qls, wos, wor, oss, ors, ls):
+                kvq, wown, wsib, xb, stage, vt, wof, ostage, obuf, sa, sb, acc,
+                wls, wss, wrs, xss, xrs, ass, ars, rss, rrs, qls, wos, wor, oss, ors, ls):
     c = lax.axis_index('cp')
     t = lax.axis_index('tp')
     i, k = t // 2, t % 2
     T, H = x_ref.shape
-    half = T // 2
     sib = {'cp': c, 'tp': i * 2 + 1 - k}
     right = {'cp': c, 'tp': ((i + 1) % nx) * 2 + k}
     left = {'cp': c, 'tp': ((i + nx - 1) % nx) * 2 + k}
     peer = [{'cp': (c + d) % cp, 'tp': t} for d in range(cp)]
     same = [{'cp': (c + dc) % cp, 'tp': ((i + di) % nx) * 2 + k} for di in range(nx) for dc in range(cp)]
     barrier_with([sib] + same[1:])
-    lo, hi = pl.ds(0, half), pl.ds(half, half)
     full = pl.ds(0, T)
 
     R = wo_ref.shape[0]
@@ -95,35 +93,54 @@
     w9 = wcopy(9, wof.at[oi * 2 + k], oi, k, rfull, sib)
 
 
+    quarter = T // 4
+
+    def part(a, b):
+        return pl.ds(a * quarter, (b - a) * quarter)
+
     def xcopy(n, src, slot, rows, dev):
         return remote(src.at[rows], xb.at[slot, rows], xss.at[n], xrs.at[n], dev)
 
-    sends = [
-        xcopy(0, x_ref, 0, lo, right), xcopy(1, x_ref, 1, hi, left),
-        xcopy(2, x_ref, 0, hi, right), xcopy(3, x_ref, 1, lo, left),
+    to_r = [
+        xcopy(0, x_ref, 0, part(0, 2), right), xcopy(1, x_ref, 0, part(2, 3), right), xcopy(2, xb.at[0], 2, part(0, 1), right),
+        xcopy(3, x_ref, 0, part(3, 4), right), xcopy(4, xb.at[0], 2, part(1, 2), right),
     ]
-    own_w = [wq_ref, wk_ref, wv_ref]
-    wsend = [remote(own_w[n], wsib.at[n], wss.at[n], wrs.at[n], sib) for n in range(3)]
-    for s in (sends[0], sends[1], *wsend, sends[2], sends[3]):
+    to_l = [
+        xcopy(5, x_ref, 1, part(2, 4), left), xcopy(6, x_ref, 1, part(1, 2), left), xcopy(7, xb.at[1], 2, part(2, 3), left),
+        xcopy(8, x_ref, 1, part(0, 1), left), xcopy(9, xb.at[1], 2, part(3, 4), left),
+    ]
+    own_h = [wq_ref, wk_ref, wv_ref]
+    wsend = [remote(own_h[n], wsib.at[n], wss.at[n], wrs.at[n], sib) for n in range(3)]
+    wload = [pltpu.make_async_copy(own_h[n], wown.at[n], wls.at[n]) for n in range(3)]
+    for s in (to_r[0], to_l[0], *wload, *wsend, to_r[1], to_l[1]):
         s.start()
 
-    pend = list(sends) + wsend
+    pend = to_r + to_l + wsend
     arrive = []
 
-    units = [(0, full), (nx - 1, lo), (1, hi), (nx - 1, hi), (1, lo), (2, lo), (2, hi)]
-
-    def compute(u, src, rows):
+    units = [
+        (0, full), (nx - 1, part(0, 2)), (1, part(2, 4)), (nx - 1, part(2, 3)), (1, part(1, 2)), (2, part(0, 1)), (2, part(2, 3)),
+        (nx - 1, part(3, 4)), (1, part(0, 1)), (2, part(1, 2)), (2, part(3, 4)),
+    ]
+
+    def compute(u, src):
+        rows = units[u][1]
         xv = src[rows, :]
         for w in range(2):
-            if u == 0 and w == 1:
-                for s in wsend:
-                    s.wait_recv()
             for n in range(3):
-                wref = own_w[n] if w == 0 else wsib.at[n]
-                r = jnp.dot(xv, wref[...], preferred_element_type=F32).astype(BF16)
+                if u == 0:
+                    (wsend[n].wait_recv if w else wload[n].wait)()
+                wref = wown if w == 0 else wsib
+                r = jnp.dot(xv, wref[n], preferred_element_type=F32).astype(BF16)
                 kk = k if w == 0 else 1 - k
                 for m in range(2):
-                    stage[u, 2 * kk + m, n, rows, :] = r[:, m * HEAD:(m + 1) * HEAD]
+                    stage[2 * kk + m, n, pl.ds(base[u], rows.size), :] = r[:, m * HEAD:(m + 1) * HEAD]
+
+    sizes = [r.size for _, r in units]
+    base = [sum(sizes[:u]) for u in range(len(units))]
+
+    def staged(u, a, n):
+        return stage.at[a, n, pl.ds(base[u], sizes[u])]
 
     def block_of(u, d):
         dj, _ = units[u]
@@ -133,13 +150,13 @@
         rows = units[u][1]
         b = block_of(u, 0)
         for d in range(1, cp):
-            cps = remote(stage.at[u, (c + d) % cp, :, rows], kvq.at[b, :, rows], ass.at[u, d], ars.at[u, d], peer[d])
+            cps = remote(staged(u, (c + d) % cp, pl.ds(0, 3)), kvq.at[b, :, rows], ass.at[u, d], ars.at[u, d], peer[d])
             cps.start()
             pend.append(cps)
-        lc = pltpu.make_async_copy(stage.at[u, c, :, rows], kvq.at[b, :, rows], qls.at[u])
+        lc = pltpu.make_async_copy(staged(u, c, pl.ds(0, 3)), kvq.at[b, :, rows], qls.at[u])
         lc.start()
         locs.append(lc)
-        relay(u, 0, stage.at[u, c, pl.ds(1, 2), rows])
+        relay(u, 0, staged(u, c, pl.ds(1, 2)))
 
     def relay(u, d, src):
         rows = units[u][1]
@@ -153,48 +170,34 @@
         rows = units[u][1]
         for d in range(1, cp):
             b = block_of(u, d)
-            remote(stage.at[u, 0, :, rows], kvq.at[b, :, rows], ass.at[u, d], ars.at[u, d], peer[d]).wait_recv()
+            remote(staged(u, 0, pl.ds(0, 3)), kvq.at[b, :, rows], ass.at[u, d], ars.at[u, d], peer[d]).wait_recv()
             relay(u, d, kvq.at[b, pl.ds(1, 2), rows])
 
     locs = []
-    compute(0, x_ref, full)
+    compute(0, x_ref)
     send(0)
     slots(cp, nx, cap, c, i, k, idx_ref, prow_ref)
-    sends[0].wait_recv()
-    f = xcopy(4, xb.at[0], 2, lo, right)
-    f.start()
-    g = xcopy(5, xb.at[1], 2, hi, left)
-    sends[1].wait_recv()
-    g.start()
-    pend += [f, g]
+    for first, rest in ((to_r[0], to_r[2:]), (to_l[0], to_l[2:])):
+        first.wait_recv()
+        for s in rest:
+            s.start()
     for w in (w0, w1, w2, w3, w6):
         w.start()
     wl.start()
-    compute(1, xb.at[0], lo)
-    send(1)
-    compute(2, xb.at[1], hi)
-    send(2)
-    pass_on(0)
-    sends[2].wait_recv()
-    compute(3, xb.at[0], hi)
-    send(3)
-    sends[3].wait_recv()
-    compute(4, xb.at[1], lo)
-    send(4)
-    pass_on(1)
-    pass_on(2)
-    f.wait_recv()
-    compute(5, xb.at[2], lo)
-    send(5)
-    g.wait_recv()
-    compute(6, xb.at[2], hi)
-    send(6)
-    for u in range(3, 7):
+    for u, src, got in ((1, 0, None), (2, 1, None), (3, 0, to_r[1]), (4, 1, to_l[1]), (5, 2, to_r[2]), (6, 2, to_l[2]),
+                        (7, 0, to_r[3]), (8, 1, to_l[3]), (9, 2, to_r[4]), (10, 2, to_l[4])):
+        if got is not None:
+            got.wait_recv()
+        compute(u, xb.at[src])
+        send(u)
+        for v in {2: (0,), 4: (1, 2), 6: (3, 4), 8: (5, 6)}.get(u, ()):
+            pass_on(v)
+    for u in range(7, 11):
         pass_on(u)
     for u, d in arrive:
         rows = units[u][1]
         b = block_of(u, d) + 1 - 2 * k
-        remote(stage.at[u, 0, pl.ds(1, 2), rows], kvq.at[b, pl.ds(1, 2), rows], rss.at[u, d], rrs.at[u, d], sib).wait_recv()
+        remote(staged(u, 0, pl.ds(1, 2)), kvq.at[b, pl.ds(1, 2), rows], rss.at[u, d], rrs.at[u, d], sib).wait_recv()
     for lc in locs:
         lc.wait()
 
@@ -450,15 +453,15 @@
         out_shape=[
             jax.ShapeDtypeStruct((T, H), BF16), jax.ShapeDtypeStruct((2, T), jnp.int32),
         ],
-        in_specs=[spec(VMEM)] * 6,
+        in_specs=[spec(VMEM)] + [spec(pl.ANY)] * 4 + [spec(VMEM)],
         out_specs=[spec(VMEM)] * 2,
         scratch_shapes=[
-            VMEM((nb, 3, T, HEAD), BF16), VMEM((3, H, W), BF16), VMEM((3, T, H), BF16), VMEM((7, 4, 3, T, HEAD), BF16),
+            VMEM((nb, 3, T, HEAD), BF16), VMEM((3, H, W), BF16), VMEM((3, H, W), BF16), VMEM((3, T, H), BF16), VMEM((4, 3, nx * T, HEAD), BF16),
             VMEM((nb // 2, HEAD, 2 * T), BF16), VMEM((tp, wo.shape[0], H), BF16),
             VMEM((2 * cp, 2, T, HEAD), BF16), VMEM((tp, T, 2 * HEAD), BF16),
             VMEM((2 * T, 2 * T), F32), VMEM((2 * T, 2 * T), F32), VMEM((HEAD, 2 * T), F32),
-            DMA((3,)), DMA((3,)), DMA((6,)), DMA((6,)),
-            DMA((7, cp)), DMA((7, cp)), DMA((7, cp)), DMA((7, cp)), DMA((7,)),
+            DMA((3,)), DMA((3,)), DMA((3,)), DMA((10,)), DMA((10,)),
+            DMA((11, cp)), DMA((11, cp)), DMA((11, cp)), DMA((11, cp)), DMA((11,)),
             DMA((10,)), DMA((10,)), DMA((2 * cp, 2)), DMA((2 * cp, 2)), DMA((2,)),
         ],
         compiler_params=params(0),

time: 238 us -> 233 us (0.979)
  Pallas kernels: 235 us -> 230 us
    pallas_call x1, Pallas kernels: 139 us -> 135 us  [experts(): pl.pallas_call(functools.partial(moe_kernel, cp, tp, cap), out_shape=jax....]
where the time goes in v5:
time: 233 us; the launch traced here: 232 us
  Pallas kernels  230 us (99%)
    pallas_call x1, Pallas kernels, experts(): pl.pallas_call(functools.partial(moe_kernel, cp, tp, cap), out_shape=jax....  135 us
    pallas_call x1, Pallas kernels, attention(): pl.pallas_call(functools.partial(attn_kernel, cp, nx, cap), out_shape=[ja...  95.2 us

profile of v5, /device:TPU:111, one launch (start us, length us, event | category | flops | bytes accessed | tf_op | source)
XLA Modules:
  0.0 232.4 jit_solution(10917779467771127469)
XLA Ops:
  0.0 95.2 %attn.1 = (bf16[256,2048]{1,0:T(8,128)(2,1)}, s32[2,256]{1,0:T(2,128)}) custom-call(bf16[256,2048]{1,0:T(8,128)(2,1)} %x_ref.1, bf16[2048,256]{1,0:T(8,128)(2,1)} %wq_ref.1, bf16[2048,256]{1,0:T(8,128)(2,1)} %wk_ref.1, bf16[2048,256]{1,0:T(8,128)(2,1)} %wv_ref.1, bf16[256,2048]{1,0:T(8,128)(2,1)} %wo_ref.1, s32[2,256]{1,0:T(2,128)} %bitcast.2), custom_call_target="tpu_custom_call" | custom-call | tf_op jit(solution)/shard_map/attn/pallas_call | solution.py:451
  95.2 134.9 %moe.1 = bf16[256,2048]{1,0:T(8,128)(2,1)} custom-call(bf16[256,2048]{1,0:T(8,128)(2,1)} %get-tuple-element.7.h_ref, s32[2,256]{1,0:T(2,128)} %get-tuple-element.8.prow_ref, f32[2,256]{1,0:T(2,128)} %bitcast.3, bf16[1,2048,1024]{2,1,0:T(8,128)(2,1)} %wg_hbm.1, bf16[1,2048,1024]{2,1,0:T(8,128)(2,1)} %wu_hbm.1, bf16[1,1024,2048]{2,1,0:T(8,128)(2,1)} %wd_hbm.1), custom_call_target="tpu_custom_call" | custom-call | tf_op jit(solution)/shard_map/moe/pallas_call | solution.py:476
  230.1 2.3 copy.12

commit v6 on v5

--- a/solution.py
+++ b/solution.py
@@ -60,7 +60,7 @@
 
 def attn_kernel(cp, nx, cap, x_ref, wq_ref, wk_ref, wv_ref, wo_ref, idx_ref, h_ref, prow_ref,
                 kvq, wown, wsib, xb, stage, vt, wof, ostage, obuf, sa, sb, acc,
-                wls, wss, wrs, xss, xrs, ass, ars, rss, rrs, qls, wos, wor, oss, ors, ls):
+                wls, wss, wrs, xss, xrs, ass, ars, rss, rrs, qls, wos, wor, oss, ors, ls, bxs, bxr, bys, byr):
     c = lax.axis_index('cp')
     t = lax.axis_index('tp')
     i, k = t // 2, t % 2
@@ -74,7 +74,7 @@
     full = pl.ds(0, T)
 
     R = wo_ref.shape[0]
-    hr = R // 2
+    hr = R // 4
     rlo, rhi, rfull = pl.ds(0, hr), pl.ds(hr, hr), pl.ds(0, R)
     ri, li, oi = (i + 1) % nx, (i + nx - 1) % nx, (i + 2) % nx
     def wcopy(n, src, chip, core, rows, to):
@@ -92,6 +92,15 @@
     w8 = wcopy(8, wof.at[ri * 2 + k], ri, k, rfull, sib)
     w9 = wcopy(9, wof.at[oi * 2 + k], oi, k, rfull, sib)
 
+
+    rq = pl.ds(R // 2 + c * (R // 2 // cp), R // 2 // cp)
+
+    def wrow(di):
+        return remote(wo_ref.at[rq], wof.at[t, rq], bxs.at[di], bxr.at[di], {'cp': c, 'tp': ((i + di) % nx) * 2 + k})
+
+    def wcol(di, d):
+        shard = ((i + nx - di) % nx) * 2 + k
+        return remote(wof.at[shard, rq], wof.at[shard, rq], bys.at[di, d], byr.at[di, d], peer[d])
 
     quarter = T // 4
 
@@ -181,7 +190,7 @@
         first.wait_recv()
         for s in rest:
             s.start()
-    for w in (w0, w1, w2, w3, w6):
+    for w in (wrow(1), wrow(nx - 1), wrow(2), w0, w1, w2, w3, w6):
         w.start()
     wl.start()
     for u, src, got in ((1, 0, None), (2, 1, None), (3, 0, to_r[1]), (4, 1, to_l[1]), (5, 2, to_r[2]), (6, 2, to_l[2]),
@@ -192,6 +201,10 @@
         send(u)
         for v in {2: (0,), 4: (1, 2), 6: (3, 4), 8: (5, 6)}.get(u, ()):
             pass_on(v)
+    for di in range(1, nx):
+        wrow(di).wait_recv()
+        for d in range(1, cp):
+            wcol(di, d).start()
     for u in range(7, 11):
         pass_on(u)
     for u, d in arrive:
@@ -282,19 +295,19 @@
             osend(n, 0).start()
             osend(n, 1).start()
 
-    run(1, 4)
-    w2.wait_recv()
-    w7.start()
-    w3.wait_recv()
-    w8.start()
-    run(4, npair)
+    run(1, 5)
+    for di in range(1, nx):
+        for d in range(1, cp):
+            wcol(di, d).wait_recv()
+    for w in (w2, w3, w4, w5):
+        w.wait_recv()
+    for w in (w7, w8, w9):
+        w.start()
+    run(5, npair)
     attend(0)
     osend(0, 1).start()
     lo_c = pltpu.make_async_copy(ostage.at[0, 0], obuf.at[i * 2 + c // 2, :, col], ls.at[1])
     lo_c.start()
-    w4.wait_recv()
-    w5.wait_recv()
-    w9.start()
     wl.wait()
     for w in (w6, w7, w8, w9):
         w.wait_recv()
@@ -317,6 +330,10 @@
 
     for w in (w0, w1, w2, w3, w4, w5, w6, w7, w8, w9):
         w.wait_send()
+    for di in range(1, nx):
+        wrow(di).wait_send()
+        for d in range(1, cp):
+            wcol(di, d).wait_send()
 
     osend(0, 1).wait_send()
 
@@ -463,6 +480,7 @@
             DMA((3,)), DMA((3,)), DMA((3,)), DMA((10,)), DMA((10,)),
             DMA((11, cp)), DMA((11, cp)), DMA((11, cp)), DMA((11, cp)), DMA((11,)),
             DMA((10,)), DMA((10,)), DMA((2 * cp, 2)), DMA((2 * cp, 2)), DMA((2,)),
+            DMA((nx,)), DMA((nx,)), DMA((nx, cp)), DMA((nx, cp)),
         ],
         compiler_params=params(0),
         name='attn',

time: 233 us -> 230 us (0.987)
  the two profiles are of different devices: /device:TPU:111 before, /device:TPU:107 now
where the time goes in v6:
time: 230 us
  Pallas kernels  227 us (99%)
    pallas_call x1, Pallas kernels, experts(): pl.pallas_call(functools.partial(moe_kernel, cp, tp, cap), out_shape=jax....  132 us
    pallas_call x1, Pallas kernels, attention(): pl.pallas_call(functools.partial(attn_kernel, cp, nx, cap), out_shape=[ja...  95.3 us

profile of v6, /device:TPU:107, one launch (start us, length us, event | category | flops | bytes accessed | tf_op | source)
XLA Modules:
  0.0 229.8 jit_solution(14051939312853626686)
XLA Ops:
  0.0 95.3 %attn.1 = (bf16[256,2048]{1,0:T(8,128)(2,1)}, s32[2,256]{1,0:T(2,128)}) custom-call(bf16[256,2048]{1,0:T(8,128)(2,1)} %x_ref.1, bf16[2048,256]{1,0:T(8,128)(2,1)} %wq_ref.1, bf16[2048,256]{1,0:T(8,128)(2,1)} %wk_ref.1, bf16[2048,256]{1,0:T(8,128)(2,1)} %wv_ref.1, bf16[256,2048]{1,0:T(8,128)(2,1)} %wo_ref.1, s32[2,256]{1,0:T(2,128)} %bitcast.2), custom_call_target="tpu_custom_call" | custom-call | tf_op jit(solution)/shard_map/attn/pallas_call | solution.py:468
  95.3 132.2 %moe.1 = bf16[256,2048]{1,0:T(8,128)(2,1)} custom-call(bf16[256,2048]{1,0:T(8,128)(2,1)} %get-tuple-element.7.h_ref, s32[2,256]{1,0:T(2,128)} %get-tuple-element.8.prow_ref, f32[2,256]{1,0:T(2,128)} %bitcast.3, bf16[1,2048,1024]{2,1,0:T(8,128)(2,1)} %wg_hbm.1, bf16[1,2048,1024]{2,1,0:T(8,128)(2,1)} %wu_hbm.1, bf16[1,1024,2048]{2,1,0:T(8,128)(2,1)} %wd_hbm.1), custom_call_target="tpu_custom_call" | custom-call | tf_op jit(solution)/shard_map/moe/pallas_call | solution.py:494
  227.5 2.3 %copy.12 = bf16[256,2048]{1,0:T(8,128)(2,1)} copy(bf16[256,2048]{1,0:T(8,128)(2,1)} %moe.1) | data formatting | bytes 2097152
